TPU v7x, 32 devices: a whole 2x2x4 slice. The times are simulated.
32 devices in a mesh: dp: 4 (over x, core), expert: 8 (over z, y).
Axes of the slice: x: 2, y: 2, z: 4, core: 2. Of those that a mesh axis runs over, the one named last changes fastest.
Arguments:
- tokens: bfloat16 [32, 1024, 768], P('dp', 'expert'), may hold values from -6 to 6
- cotangent: bfloat16 [32, 1024, 768], P('dp', 'expert'), may hold values from -6 to 6
- w_project: bfloat16 [768, 2304], replicated, may hold values from -0.21875 to 0.21875
- w_output: bfloat16 [768, 768], replicated, may hold values from -0.875 to 0.875
- norm_gain: float32 [2, 768], replicated, may hold values from 0.5 to 1.5
- norm_bias: float32 [2, 768], replicated, may hold values from -3 to 3
- router: float32 [768, 8], replicated, may hold values from -0.21875 to 0.21875
- expert_weights: bfloat16 [8, 2, 768, 3072], P('expert'), may hold values from -0.21875 to 0.21875
- routes: int32 [32, 1024, 2], P('dp', 'expert'), may hold values from 0 to 7, all different within a row; in each aligned block of 128 rows (0 to 127, 128 to 255, ..., all dimensions but the last counted through in order) at most 40 rows name the same one
- keep_mask: int32 [32, 1024, 2], P('dp', 'expert'), may hold values 0 or 1
- frozen: int32 [8], replicated, may hold values from 0 to 1, as said below
- owner_list: int32 [8], replicated, may hold values from 0 to 7, each once
- attend_master: float32 [8, 768, 384], P('expert'), may hold values from -0.21875 to 0.21875
- attend_first: float32 [8, 768, 384], P('expert'), may hold values from -32 to 32
- attend_second: float32 [8, 768, 384], P('expert'), may hold values from 78.6432 to 1245.184
- attend_left: float32 [8, 768, 768], P('expert'), may hold values from -1 to 1
- attend_right: float32 [8, 384, 384], P('expert'), may hold values from -1 to 1
- expert_master: float32 [8, 2, 768, 3072], P('expert', None, None, 'dp'), may hold values from -0.21875 to 0.21875
- expert_first: float32 [8, 2, 768, 3072], P('expert', None, None, 'dp'), may hold values from -20 to 20
- expert_second: float32 [8, 2, 768, 3072], P('expert', None, None, 'dp'), may hold values from 26.2144 to 425.984
- expert_average: float32 [8, 2, 768, 3072], P('expert', None, None, 'dp'), may hold values from -0.21875 to 0.21875
- expert_basis: float32 [8, 768, 768], P('expert'), may hold values from -1 to 1
- router_first: float32 [768, 8], replicated, may hold values from -640 to 640
- router_second: float32 [768, 8], replicated, may hold values from 21299.2 to 344064
- norm_first: float32 [4, 768], replicated, may hold values from -128 to 128
- norm_second: float32 [4, 768], replicated, may hold values from 851.968 to 13762.56
Outputs:
- output: bfloat16 [32, 1024, 768], P('dp', 'expert')
- input_grad: bfloat16 [32, 1024, 768], P('dp', 'expert')
- norm_grad: float32 [4, 768], replicated
- norm_new: float32 [4, 768], replicated
- norm_first_new: float32 [4, 768], replicated
- norm_second_new: float32 [4, 768], replicated
- router_grad: float32 [768, 8], replicated
- router_new: float32 [768, 8], replicated
- router_first_new: float32 [768, 8], replicated
- router_second_new: float32 [768, 8], replicated
- attend_grad: float32 [8, 768, 384], P('expert')
- attend_master_new: float32 [8, 768, 384], P('expert')
- attend_first_new: float32 [8, 768, 384], P('expert')
- attend_second_new: float32 [8, 768, 384], P('expert')
- expert_grad: float32 [8, 2, 768, 3072], P('expert', None, None, 'dp')
- expert_master_new: float32 [8, 2, 768, 3072], P('expert', None, None, 'dp')
- expert_first_new: float32 [8, 2, 768, 3072], P('expert', None, None, 'dp')
- expert_second_new: float32 [8, 2, 768, 3072], P('expert', None, None, 'dp')
- expert_average_new: float32 [8, 2, 768, 3072], P('expert', None, None, 'dp')
Inputs may be any that keep to these rules, and one draw needn't show every extreme that they name: `routes`: each token names two different experts. In each aligned block of 128 tokens (one sequence's tokens on one index of expert) no expert is named by more than 40 choices, and some block reaches 40. `frozen`: exactly half of the experts are flagged 1. `owner_list`: A permutation.
All inputs are finite; a program needn't handle non-finite values. No bound on the sum of `keep_mask` on one device may be relied on, other than what follows from the above.
Results may differ from a plain program's by a relative error of at most 0.025.
Values may be sent and summed in bfloat16 or wider, within the bound.
A program may use at most 448 MiB of HBM per device.

v0:
```python
import functools

import jax
import jax.numpy as jnp
from jax import lax
from jax.experimental import pallas as pl
from jax.experimental.pallas import tpu as pltpu
from jax.sharding import PartitionSpec as P


HEADS = 12
HEAD_DIM = 64
TOP = 2
TILE = 256
CHUNK = 512
ROOT = 0.7978845608028654
CUBIC = 0.044715


norm_epsilon = 1e-05
beta_one = 0.9
beta_two = 0.95
adam_epsilon = 1e-08
adam_step = 10.0
matrix_rate = 0.1
small_rate = 0.5
average_keep = 0.9
precise = lax.Precision.HIGHEST
wide = jnp.float32
low = jnp.bfloat16


def norm_parts(values):
    center = values - jnp.mean(values, axis=-1, keepdims=True)
    spread = lax.rsqrt(jnp.mean(center * center, axis=-1, keepdims=True) + norm_epsilon)
    return center * spread, spread


def norm_back(grad, normal, spread, gain_row):
    g = grad * gain_row
    moved = spread * (
        g
        - jnp.mean(g, axis=-1, keepdims=True)
        - normal * jnp.mean(g * normal, axis=-1, keepdims=True)
    )
    return moved, jnp.sum(grad * normal, axis=0), jnp.sum(grad, axis=0)


def adam_move(gradient, first_moment, second_moment):
    first_new = beta_one * first_moment + (1.0 - beta_one) * gradient
    second_new = beta_two * second_moment + (1.0 - beta_two) * gradient * gradient
    direction = (
        first_new
        / (1.0 - beta_one**adam_step)
        / (jnp.sqrt(second_new / (1.0 - beta_two**adam_step)) + adam_epsilon)
    )
    return (first_new, second_new, direction)


def dot_low(a, b, dims):
    return lax.dot_general(a.astype(low), b.astype(low), (dims, ((), ())), preferred_element_type=wide)


ROW_COL = ((1,), (0,))
ROW_ROW = ((1,), (1,))
COL_COL = ((0,), (0,))


def key_pieces(step, tile, key_len, whole):
    if whole:
        return ((0, step * tile, False), (step * tile, (step + 1) * tile, True))
    return ((0, key_len, True),)


def allowed_at(first_query, first_key, tile, key_count):
    rows = lax.broadcasted_iota(jnp.int32, (tile, key_count), 0) + first_query
    columns = lax.broadcasted_iota(jnp.int32, (tile, key_count), 1) + first_key
    return columns <= rows


def attend_kernel(whole, start_ref, q_ref, k_ref, v_ref, out_ref, log_ref):
    rows, lanes = q_ref.shape
    key_len = k_ref.shape[0]
    lane = lax.broadcasted_iota(jnp.int32, (1, lanes), 1)
    for step in range(rows // TILE):
        at = slice(step * TILE, (step + 1) * TILE)
        total, logs = None, []
        for head in range(2):
            mine = (lane // HEAD_DIM) == head
            query = jnp.where(mine, q_ref[at, :] * HEAD_DIM ** (-0.5), 0).astype(low)
            parts = []
            for first, last, masked in key_pieces(step, TILE, key_len, whole):
                if last > first:
                    scores = dot_low(query, k_ref[first:last, :], ROW_ROW)
                    if masked:
                        origin = step * TILE + (0 if whole else start_ref[0])
                        scores = jnp.where(
                            allowed_at(origin, first, TILE, last - first), scores, -1e30
                        )
                    parts.append((first, last, scores))
            top = functools.reduce(
                jnp.maximum, [jnp.max(s, axis=-1, keepdims=True) for _, _, s in parts]
            )
            summed, acc = None, None
            for first, last, scores in parts:
                weights = jnp.exp(scores - top)
                here = jnp.sum(weights, axis=-1, keepdims=True)
                values = jnp.where(mine, v_ref[first:last, :], 0).astype(low)
                add = dot_low(weights, values, ROW_COL)
                summed = here if summed is None else summed + here
                acc = add if acc is None else acc + add
            acc = acc / summed
            total = acc if total is None else total + acc
            logs.append(top + jnp.log(summed))
        out_ref[at, :] = total.astype(out_ref.dtype)
        log_ref[at, :] = jnp.where(lane < HEAD_DIM, logs[0], logs[1])


def attend_back_kernel(
    whole, start_ref, q_ref, k_ref, v_ref, g_ref, a_ref, log_ref, dq_ref, dk_ref, dv_ref, dk_sum, dv_sum
):
    rows, lanes = q_ref.shape
    key_len = k_ref.shape[0]
    lane = lax.broadcasted_iota(jnp.int32, (1, lanes), 1)
    dk_sum[...] = jnp.zeros_like(dk_sum)
    dv_sum[...] = jnp.zeros_like(dv_sum)
    for step in range(rows // TILE):
        at = slice(step * TILE, (step + 1) * TILE)
        grad_all = g_ref[at, :]
        product = grad_all.astype(wide) * a_ref[at, :].astype(wide)
        dq = None
        for head in range(2):
            mine = (lane // HEAD_DIM) == head
            query = jnp.where(mine, q_ref[at, :] * HEAD_DIM ** (-0.5), 0).astype(low)
            grad = jnp.where(mine, grad_all, 0).astype(low)
            delta = jnp.sum(jnp.where(mine, product, 0.0), axis=-1, keepdims=True)
            log_total = log_ref[at, head * HEAD_DIM : head * HEAD_DIM + 1]
            for first, last, masked in key_pieces(step, TILE, key_len, whole):
                if last > first:
                    keys, values = k_ref[first:last, :], v_ref[first:last, :]
                    weights = jnp.exp(dot_low(query, keys, ROW_ROW) - log_total)
                    if masked:
                        origin = step * TILE + (0 if whole else start_ref[0])
                        weights = jnp.where(
                            allowed_at(origin, first, TILE, last - first), weights, 0.0
                        )
                    moved = (weights * (dot_low(grad, values, ROW_ROW) - delta)).astype(low)
                    dv_sum[first:last, :] += dot_low(weights, grad, COL_COL)
                    dk_sum[first:last, :] += dot_low(moved, query, COL_COL)
                    add = dot_low(moved, jnp.where(mine, keys, 0), ROW_COL)
                    dq = add if dq is None else dq + add
        dq_ref[at, :] = (dq * HEAD_DIM ** (-0.5)).astype(low)
    dk_ref[...] = dk_sum[...].astype(low)
    dv_ref[...] = dv_sum[...].astype(low)


def head_block(rows, first):
    return pl.BlockSpec((rows, 2 * HEAD_DIM), lambda pair: (0, first + pair))


def attend(start, queries, keys, values, firsts, whole):
    rows, key_len, pairs = queries.shape[0], keys.shape[0], HEADS // 2
    width = HEADS * HEAD_DIM
    cost = 4 * rows * key_len * width // (2 if whole else 1)
    return pl.pallas_call(
        functools.partial(attend_kernel, whole),
        grid=(pairs,),
        out_shape=(
            jax.ShapeDtypeStruct((rows, width), low),
            jax.ShapeDtypeStruct((rows, width), wide),
        ),
        in_specs=[
            pl.BlockSpec(memory_space=pltpu.SMEM),
            head_block(rows, firsts[0]),
            head_block(key_len, firsts[1]),
            head_block(key_len, firsts[2]),
        ],
        out_specs=(head_block(rows, 0), head_block(rows, 0)),
        cost_estimate=pl.CostEstimate(
            flops=cost, bytes_accessed=12 * rows * width, transcendentals=rows * key_len * HEADS
        ),
        name="attend",
    )(start, queries, keys, values)


def attend_back(start, queries, keys, values, firsts, grads, attended, logs, whole):
    rows, key_len, pairs = queries.shape[0], keys.shape[0], HEADS // 2
    width = HEADS * HEAD_DIM
    cost = 10 * rows * key_len * width // (2 if whole else 1)
    return pl.pallas_call(
        functools.partial(attend_back_kernel, whole),
        grid=(pairs,),
        out_shape=(
            jax.ShapeDtypeStruct((rows, width), low),
            jax.ShapeDtypeStruct((key_len, width), low),
            jax.ShapeDtypeStruct((key_len, width), low),
        ),
        in_specs=[
            pl.BlockSpec(memory_space=pltpu.SMEM),
            head_block(rows, firsts[0]),
            head_block(key_len, firsts[1]),
            head_block(key_len, firsts[2]),
            head_block(rows, 0),
            head_block(rows, 0),
            head_block(rows, 0),
        ],
        out_specs=(head_block(rows, 0), head_block(key_len, 0), head_block(key_len, 0)),
        scratch_shapes=[
            pltpu.VMEM((key_len, 2 * HEAD_DIM), wide),
            pltpu.VMEM((key_len, 2 * HEAD_DIM), wide),
        ],
        cost_estimate=pl.CostEstimate(
            flops=cost, bytes_accessed=20 * rows * width, transcendentals=rows * key_len * HEADS
        ),
        name="attend_back",
    )(start, queries, keys, values, grads, attended, logs)


def expert_kernel(x_ref, u_ref, w_ref, act_ref, grad_ref, input_ref, gate_grad_ref):
    x = x_ref[...]
    inputs, gate_grad = None, None
    hidden = w_ref.shape[3]
    for first in range(0, hidden, CHUNK):
        at = slice(first, first + CHUNK)
        w = w_ref[0, 0, :, at]
        v = dot_low(x, w, ROW_COL)
        u = u_ref[:, at].astype(wide)
        square = v * v
        t = jnp.tanh(ROOT * v * (1.0 + CUBIC * square))
        half = 0.5 * (1.0 + t)
        act = v * half
        slope = half + 0.5 * ROOT * v * (1.0 - t * t) * (1.0 + 3.0 * CUBIC * square)
        grad = (u * slope).astype(low)
        act_ref[:, at] = act.astype(low)
        grad_ref[:, at] = grad
        here = jnp.sum(act * u, axis=-1, keepdims=True)
        add = dot_low(grad, w, ROW_ROW)
        gate_grad = here if gate_grad is None else gate_grad + here
        inputs = add if inputs is None else inputs + add
    input_ref[...] = inputs.astype(low)
    gate_grad_ref[...] = gate_grad


def expert_stage(x, u, w):
    rows, width = x.shape
    hidden = w.shape[3]

    def row_block(columns):
        return pl.BlockSpec((TILE, columns), lambda i: (i, 0))

    return pl.pallas_call(
        expert_kernel,
        grid=(rows // TILE,),
        out_shape=(
            jax.ShapeDtypeStruct((rows, hidden), low),
            jax.ShapeDtypeStruct((rows, hidden), low),
            jax.ShapeDtypeStruct((rows, width), low),
            jax.ShapeDtypeStruct((rows, 1), wide),
        ),
        in_specs=[
            row_block(width),
            row_block(hidden),
            pl.BlockSpec((1, 1, width, hidden), lambda i: (0, 0, 0, 0)),
        ],
        out_specs=(row_block(hidden), row_block(hidden), row_block(width), row_block(1)),
        cost_estimate=pl.CostEstimate(
            flops=4 * rows * width * hidden,
            bytes_accessed=6 * rows * hidden,
            transcendentals=rows * hidden,
        ),
        name="expert_stage",
    )(x, u, w)


def refresh_kernel(count, flag_ref, basis_ref, turned_ref, *refs):
    terms = [functools.reduce(jnp.add, [r[...].astype(wide) for r in refs[i : i + count]]) for i in (0, count)]
    master_ref, first_ref, second_ref, average_ref = refs[2 * count : 2 * count + 4]
    grad_out, master_out, first_out, second_out, average_out = refs[2 * count + 4 :]
    is_frozen = flag_ref[0] > 0
    grad = jnp.where(pl.program_id(0) == 0, terms[0], terms[1])
    grad_out[0, 0] = grad
    first_new, second_new, move = adam_move(
        dot_low(turned_ref[...], grad, ROW_COL), first_ref[0, 0], second_ref[0, 0]
    )
    master_new = master_ref[0, 0] - matrix_rate * dot_low(basis_ref[...], move, ROW_COL)
    master_new = jnp.where(is_frozen, master_ref[0, 0], master_new)
    master_out[0, 0] = master_new
    first_out[0, 0] = jnp.where(is_frozen, first_ref[0, 0], first_new)
    second_out[0, 0] = jnp.where(is_frozen, second_ref[0, 0], second_new)
    average_out[0, 0] = average_keep * average_ref[0, 0] + (1.0 - average_keep) * master_new


def refresh(flag, basis, terms, master, first, second, average):
    count = len(terms[0])
    _, mats, width, columns = master.shape
    step = 256 if columns % 256 == 0 else 128
    block = pl.BlockSpec((1, 1, width, step), lambda i, j: (0, i, 0, j))
    square = pl.BlockSpec((width, width), lambda i, j: (0, 0))
    return pl.pallas_call(
        functools.partial(refresh_kernel, count),
        grid=(mats, columns // step),
        out_shape=(jax.ShapeDtypeStruct(master.shape, wide),) * 5,
        in_specs=[
            pl.BlockSpec(memory_space=pltpu.SMEM),
            square,
            square,
        ]
        + [pl.BlockSpec((width, step), lambda i, j: (0, jnp.where(i == 0, j, columns // step - 1)))]
        * count
        + [pl.BlockSpec((width, step), lambda i, j: (0, jnp.where(i == 0, 0, j)))] * count
        + [block] * 4,
        out_specs=(block,) * 5,
        cost_estimate=pl.CostEstimate(
            flops=4 * mats * width * width * columns,
            bytes_accessed=38 * mats * width * columns,
            transcendentals=0,
        ),
        name="refresh",
    )(flag, basis, basis.T, *terms[0], *terms[1], master, first, second, average)


def deal_kernel(which_ref, block_ref, small_ref, out_ref):
    width = block_ref.shape[1]
    out_ref[0, :, :width] = block_ref[...]
    out_ref[0, :, width:] = small_ref[...]


def deal(which, rows, block_width, count):
    height, total = rows.shape
    extra = total - block_width * count
    if block_width % 128:
        return jnp.stack(
            [
                jnp.concatenate(
                    [
                        lax.dynamic_slice_in_dim(rows, which[s] * block_width, block_width, 1),
                        rows[:, total - extra :],
                    ],
                    axis=1,
                )
                for s in range(count)
            ]
        )
    return pl.pallas_call(
        deal_kernel,
        grid_spec=pltpu.PrefetchScalarGridSpec(
            num_scalar_prefetch=1,
            grid=(count,),
            in_specs=[
                pl.BlockSpec((height, block_width), lambda s, which: (0, which[s])),
                pl.BlockSpec((height, extra), lambda s, which: (0, total // extra - 1)),
            ],
            out_specs=pl.BlockSpec((1, height, block_width + extra), lambda s, which: (s, 0, 0)),
        ),
        out_shape=jax.ShapeDtypeStruct((count, height, block_width + extra), rows.dtype),
        name="deal",
    )(which, rows, rows)


def trade_kernel(count, in_ref, out_ref, landed, send_sem, recv_sem):
    me = lax.axis_index("expert")
    barrier = pltpu.get_barrier_semaphore()
    for shift in range(1, count):
        peer = lax.rem(me + shift, count)
        pl.semaphore_signal(
            barrier, inc=1, device_id={"expert": peer}, device_id_type=pl.DeviceIdType.MESH
        )
    pl.semaphore_wait(barrier, count - 1)
    copies = []
    for shift in range(1, count):
        peer = lax.rem(me + shift, count)
        copy = pltpu.make_async_remote_copy(
            src_ref=in_ref.at[peer],
            dst_ref=landed.at[me],
            send_sem=send_sem.at[shift - 1],
            recv_sem=recv_sem.at[shift - 1],
            device_id={"expert": peer},
            device_id_type=pl.DeviceIdType.MESH,
        )
        copy.start()
        copies.append(copy)
    for shift, copy in zip(range(1, count), copies):
        copy.wait()
        source = lax.rem(me + count - shift, count)
        out_ref[pl.ds(source, 1)] = landed[pl.ds(source, 1)]
    out_ref[pl.ds(me, 1)] = in_ref[pl.ds(me, 1)]


def trade(value):
    count, size = value.shape
    lines = -(-size // 1024) * 8
    padded = jnp.pad(value, ((0, 0), (0, lines * 128 - size))).reshape(count, lines, 128)
    out = pl.pallas_call(
        functools.partial(trade_kernel, count),
        out_shape=jax.ShapeDtypeStruct(padded.shape, padded.dtype),
        in_specs=[pl.BlockSpec(memory_space=pltpu.VMEM)],
        out_specs=pl.BlockSpec(memory_space=pltpu.VMEM),
        scratch_shapes=[
            pltpu.VMEM(padded.shape, padded.dtype),
            pltpu.SemaphoreType.DMA((count - 1,)),
            pltpu.SemaphoreType.DMA((count - 1,)),
        ],
        compiler_params=pltpu.CompilerParams(collective_id=0, has_side_effects=True),
        name="trade",
    )(padded)
    return out.reshape(count, lines * 128)[:, :size]


def send_kernel(count, capacity, code_ref, row_ref, out_ref):
    place = lax.broadcasted_iota(jnp.int32, (count * capacity, row_ref.shape[0]), 0)
    hit = jnp.logical_or(place == code_ref[0, 0:1, :], place == code_ref[0, 1:2, :])
    rows = dot_low(hit.astype(wide), row_ref[...], ROW_COL)
    for e in range(count):
        out_ref[e, 0] = rows[e * capacity : (e + 1) * capacity].astype(low)


def send_rows(code, rows, count, capacity):
    blocks, _, row_len = code.shape
    width = rows.shape[1]
    return pl.pallas_call(
        functools.partial(send_kernel, count, capacity),
        grid=(blocks,),
        out_shape=jax.ShapeDtypeStruct((count, blocks, capacity, width), low),
        in_specs=[
            pl.BlockSpec((1, TOP, row_len), lambda j: (j, 0, 0)),
            pl.BlockSpec((row_len, width), lambda j: (j, 0)),
        ],
        out_specs=pl.BlockSpec((count, 1, capacity, width), lambda j: (0, j, 0, 0)),
        cost_estimate=pl.CostEstimate(
            flops=2 * blocks * count * capacity * row_len * width,
            bytes_accessed=2 * blocks * (count * capacity + row_len) * width,
            transcendentals=0,
        ),
        name="send_rows",
    )(code, rows)


def after(value, *others):
    return lax.optimization_barrier((value, *others))[0]


def on_device(
    tokens,
    cotangent,
    w_project,
    w_output,
    norm_gain,
    norm_bias,
    router,
    expert_weights,
    routes,
    keep_mask,
    frozen,
    owner_list,
    attend_master,
    attend_first,
    attend_second,
    attend_left,
    attend_right,
    expert_master,
    expert_first,
    expert_second,
    expert_average,
    expert_basis,
    router_first,
    router_second,
    norm_first,
    norm_second,
):
    seq_dev, row_len, model_width = tokens.shape
    expert_count = lax.axis_size("expert")
    dp_count = lax.axis_size("dp")
    my_index = lax.axis_index("expert")
    row_count = seq_dev * row_len
    capacity = max(2, 5 * row_len * TOP // (4 * expert_count))
    expert_total = router.shape[1]
    slots = expert_total * capacity
    parts = expert_count // seq_dev
    whole = parts == 1
    groups, across = None, None
    if not whole:
        groups = [[p * seq_dev + s for s in range(seq_dev)] for p in range(parts)]
        across = [[p * seq_dev + s for p in range(parts)] for s in range(seq_dev)]

    def swap(value):
        return lax.all_to_all(
            value, "expert", split_axis=0, concat_axis=0, tiled=True, axis_index_groups=groups
        )

    def ring(value):
        size = value.shape[0]
        me = my_index % size
        rows = [lax.dynamic_index_in_dim(value, me, 0, keepdims=False)]
        for shift in range(1, size):
            given = lax.dynamic_index_in_dim(value, (me + shift) % size, 0, keepdims=False)
            moves = [
                (d, d - d % size + (d % size + shift) % size) for d in range(expert_count)
            ]
            rows.append(lax.ppermute(given, "expert", moves))
        return rows

    def ring_place(rows):
        size = len(rows)
        rows = jnp.stack(rows[::-1])
        first = size - 1 - my_index % size
        return lax.dynamic_slice_in_dim(jnp.concatenate([rows, rows]), first, size, 0)

    lines = dp_count // 2
    line = lax.axis_index("dp") // 2
    core = lax.axis_index("dp") % 2

    def dp_move(value, shift):
        return lax.ppermute(value, "dp", [(d, (d + 2 * shift) % dp_count) for d in range(dp_count)])

    def other_core(value):
        return lax.ppermute(value, "dp", [(d, d ^ 1) for d in range(dp_count)])

    def cut_dp(value, axis, side):
        size = value.shape[axis] // dp_count
        return [
            lax.dynamic_slice_in_dim(
                value, ((line + shift) % lines * 2 + side) * size, size, axis
            )
            for shift in range(lines)
        ]

    def halve(value, axis, given):
        return [
            (mine.astype(wide) + other_core(theirs).astype(wide)).astype(low)
            for mine, theirs in zip(cut_dp(value, axis, core), given)
        ]

    def spread(half):
        return [half[0]] + [dp_move(half[shift], shift) for shift in range(1, lines)]

    def gather_dp(value):
        rows = jnp.stack([value] + [dp_move(value, shift) for shift in range(1, lines)])
        others = other_core(rows)
        out = jnp.zeros((dp_count,) + value.shape, value.dtype)
        for shift in range(lines):
            first = (line + lines - shift) % lines * 2
            out = lax.dynamic_update_index_in_dim(out, rows[shift], first + core, 0)
            out = lax.dynamic_update_index_in_dim(out, others[shift], first + 1 - core, 0)
        return out.reshape((-1,) + value.shape[1:])

    def exchange(value):
        return lax.all_to_all(value, "expert", split_axis=0, concat_axis=0, tiled=True)

    token_seq = swap(tokens)
    token_rows = token_seq.reshape(row_count, model_width).astype(wide)

    choice_ids = routes.reshape(seq_dev, row_len * TOP)
    onehot = choice_ids[..., None] == jnp.arange(expert_total, dtype=jnp.int32)
    before_me = jnp.tri(row_len * TOP, k=-1, dtype=low)
    earlier = jnp.einsum("pq,sqe->spe", before_me, onehot.astype(low), preferred_element_type=wide)
    slot_index = jnp.sum(jnp.where(onehot, earlier, 0.0), axis=-1).astype(jnp.int32)
    place = choice_ids * capacity + slot_index
    home_code = jnp.where(keep_mask.reshape(choice_ids.shape) > 0, place, -1 - choice_ids)
    home_code = jnp.swapaxes(home_code.reshape(seq_dev, row_len, TOP), 1, 2)
    code = ring_place(ring(home_code))

    def hits_of(codes):
        return [
            codes[:, k, :, None] == jnp.arange(slots, dtype=jnp.int32) for k in range(TOP)
        ]

    cot_slots = send_rows(
        home_code, cotangent.reshape(row_count, model_width), expert_total, capacity
    )
    cot_back = exchange(after(cot_slots, token_seq))
    normal_one, spread_one = norm_parts(token_rows)
    low_one = (normal_one * norm_gain[0] + norm_bias[0]).astype(low)
    projected = jnp.dot(low_one, w_project, preferred_element_type=wide).astype(low)
    start = ((my_index // seq_dev) * row_count).astype(jnp.int32).reshape(1)
    pairs = HEADS // 2
    if whole:
        key_value, firsts = projected, (0, pairs, 2 * pairs)
    else:
        key_value = lax.all_gather(
            projected[:, model_width:], "expert", axis=0, tiled=True, axis_index_groups=across
        )
        firsts = (0, 0, pairs)
    attended_low, logs = attend(start, projected, key_value, key_value, firsts, whole)
    middle = token_rows + jnp.dot(attended_low, w_output, preferred_element_type=wide)
    normal_two, spread_two = norm_parts(middle)
    low_two = (normal_two * norm_gain[1] + norm_bias[1]).astype(low)

    hits = hits_of(code)
    sending = send_rows(code, low_two, expert_total, capacity)
    received = exchange(after(sending, cot_back))
    cot_rows = jnp.swapaxes(
        cot_back.reshape(parts, seq_dev, seq_dev, capacity, model_width), 1, 2
    ).reshape(-1, model_width)
    w_second = expert_weights[0, 1]
    pulled = jnp.dot(cot_rows, w_second, preferred_element_type=wide).astype(low)
    received = received.reshape(-1, model_width)

    low_two_wide = low_two.astype(wide)
    logits = jnp.dot(low_two_wide, router, precision=precise).reshape(
        seq_dev, 1, row_len, expert_total
    )
    route = jnp.where(code >= 0, code // capacity, -1 - code)
    onehot_four = (route[..., None] == jnp.arange(expert_total, dtype=jnp.int32)).astype(wide)
    gates = jax.nn.softmax(jnp.sum(onehot_four * logits, axis=-1), axis=1)
    gate_slots = sum(
        jnp.sum(jnp.where(hits[k], gates[:, k, :, None], 0.0), axis=1) for k in range(TOP)
    )
    gate_slots = jnp.swapaxes(gate_slots.reshape(seq_dev, expert_total, capacity), 0, 1)
    gate_slots = gate_slots.reshape(expert_total, seq_dev * capacity)
    select = sum(jnp.where(hits[k], gates[:, k, :, None], 0.0) for k in range(TOP)).astype(low)
    select = select.reshape(seq_dev, row_len, expert_total, capacity)
    cot_seq = swap(after(cotangent, received, pulled, gate_slots))
    grad_final = cot_seq.reshape(row_count, model_width).astype(wide)

    activated_low, grad_before, grad_inputs, gate_grad = expert_stage(
        received, pulled, expert_weights
    )
    slot_shape = (expert_count, seq_dev, capacity)
    grad_inputs = grad_inputs.reshape(slot_shape + (model_width,))
    pair_slots = seq_dev * capacity
    traded = trade(
        jnp.concatenate([gate_slots, gate_grad.reshape(expert_count, pair_slots)], axis=1)
    )
    grad_inputs, activated_low, grad_before, traded, _ = lax.optimization_barrier(
        (grad_inputs, activated_low, grad_before, traded, cot_seq)
    )
    gate_rows = traded[:, :pair_slots].reshape(-1, 1)
    gate_grad_home = traded[:, pair_slots:]
    grad_home = exchange(grad_inputs)
    result = jnp.einsum(
        "rf,df->rd", activated_low, w_second, preferred_element_type=wide
    ).astype(low)
    grad_flat = (gate_rows * cot_rows.astype(wide)).astype(low)
    input_flat = (gate_rows * received.astype(wide)).astype(low)
    grad_first_w = jnp.einsum("rd,rf->df", input_flat, grad_before, preferred_element_type=wide)
    grad_second_w = jnp.einsum("rd,rf->df", grad_flat, activated_low, preferred_element_type=wide)
    flag_value = jnp.sum(
        frozen * (jnp.arange(frozen.shape[0], dtype=jnp.int32) == my_index).astype(jnp.int32)
    )
    trainable = (1 - flag_value).astype(wide)
    expert_grads = [(grad * trainable).astype(low) for grad in (grad_first_w, grad_second_w)]
    expert_given = [cut_dp(grad, 1, 1 - core) for grad in expert_grads]
    coming_back = exchange(after(result.reshape(slot_shape + (model_width,)), grad_home, expert_given))
    expert_half = [halve(grad, 1, given) for grad, given in zip(expert_grads, expert_given)]
    expert_terms = [spread(half) for half in expert_half]

    gate_grad_flat = jnp.swapaxes(
        gate_grad_home.reshape(expert_count, seq_dev, capacity), 0, 1
    ).reshape(seq_dev, 1, slots)
    grad_gate = jnp.stack(
        [jnp.sum(jnp.where(hits[k], gate_grad_flat, 0.0), axis=-1) for k in range(TOP)], axis=1
    )
    grad_chosen = gates * (grad_gate - jnp.sum(gates * grad_gate, axis=1, keepdims=True))
    grad_logits = jnp.sum(onehot_four * grad_chosen[..., None], axis=1).reshape(
        row_count, expert_total
    )
    router_local = jnp.dot(low_two_wide.T, grad_logits, precision=precise)
    grad_low_two = jnp.dot(grad_logits, router.T, precision=precise) + jnp.einsum(
        "jtec,ejcd->jtd", select, grad_home, preferred_element_type=wide
    ).reshape(row_count, model_width)
    moved_two, gain_two, bias_two = norm_back(grad_low_two, normal_two, spread_two, norm_gain[1])
    grad_middle = grad_final + moved_two
    grad_branch = grad_middle.astype(low)
    grad_w_output = jnp.einsum("rd,re->de", attended_low, grad_branch, preferred_element_type=wide)
    grad_attended = jnp.einsum("re,de->rd", grad_branch, w_output, preferred_element_type=wide).astype(
        low
    )

    grad_attended = after(grad_attended, expert_half)
    grad_query, grad_keys, grad_values = attend_back(
        start, projected, key_value, key_value, firsts, grad_attended, attended_low, logs, whole
    )
    mixture = jnp.einsum("jtec,ejcd->jtd", select, after(coming_back, grad_query), preferred_element_type=wide)
    output_seq = (
        (middle + mixture.reshape(row_count, model_width))
        .astype(low)
        .reshape(seq_dev, row_len, model_width)
    )
    if not whole:
        grad_keys, grad_values = (
            lax.psum_scatter(
                g, "expert", scatter_dimension=0, tiled=True, axis_index_groups=across
            )
            for g in (grad_keys, grad_values)
        )
    grad_projected = jnp.concatenate([grad_query, grad_keys, grad_values], axis=1)
    grad_low_one = jnp.einsum("re,de->rd", grad_projected, w_project, preferred_element_type=wide)
    moved_one, gain_one, bias_one = norm_back(grad_low_one, normal_one, spread_one, norm_gain[0])
    input_grad = (grad_middle + moved_one).astype(low).reshape(seq_dev, row_len, model_width)
    input_grad = swap(after(input_grad, coming_back, expert_terms))

    grad_w_project = jnp.einsum("rd,re->de", low_one, grad_projected, preferred_element_type=wide)
    grad_norms = jnp.stack([gain_one, gain_two, bias_one, bias_two])
    block_width = attend_master.shape[2]
    expert_grad, expert_master_new, expert_first_new, expert_second_new, expert_average_new = refresh(
        flag_value.astype(jnp.int32).reshape(1),
        expert_basis[0].astype(low),
        expert_terms,
        expert_master,
        expert_first,
        expert_second,
        expert_average,
    )

    slot_range = jnp.arange(expert_count, dtype=jnp.int32)
    which_block = jnp.sum(
        slot_range[None, :] * (owner_list[None, :] == slot_range[:, None]).astype(jnp.int32), axis=1
    )
    small_width = expert_total + 4
    small = jnp.concatenate([router_local, grad_norms.T], axis=1).astype(low)
    small = jnp.pad(small, ((0, 0), (0, 128 - small_width)))
    grad_full = jnp.concatenate(
        [grad_w_project.astype(low), grad_w_output.astype(low), small], axis=1
    )
    half_rows = halve(grad_full, 0, cut_dp(grad_full, 0, 1 - core))
    my_rows = sum(term.astype(wide) for term in spread(half_rows)).astype(low)
    my_rows = deal(which_block, my_rows, block_width, expert_count)
    my_rows = after(exchange(after(my_rows, input_grad)), expert_grad)
    my_rows_done = my_rows
    my_rows = jnp.sum(my_rows.astype(wide), axis=0)
    summed = gather_dp(my_rows.astype(low)).astype(wide)
    block_grad = summed[:, :block_width]
    small_sum = summed[:, block_width : block_width + small_width]
    router_grad = small_sum[:, :expert_total]
    norm_grad = small_sum[:, expert_total:].T

    left_basis = attend_left[0].astype(low)
    right_basis = attend_right[0].astype(low)
    rotated = dot_low(dot_low(left_basis, block_grad, COL_COL), right_basis, ROW_COL)
    attend_first_new, attend_second_new, direction = adam_move(
        rotated, attend_first[0], attend_second[0]
    )
    stepped = dot_low(dot_low(left_basis, direction, ROW_COL), right_basis, ROW_ROW)
    attend_master_new = attend_master[0] - matrix_rate * stepped

    output = swap(after(output_seq, my_rows_done))

    output = after(output, attend_master_new)

    router_first_new, router_second_new, router_step = adam_move(
        router_grad, router_first, router_second
    )
    router_new = router - matrix_rate * router_step
    norm_params = jnp.concatenate([norm_gain, norm_bias], axis=0)
    norm_first_new, norm_second_new, norm_step = adam_move(norm_grad, norm_first, norm_second)
    norm_new = norm_params - small_rate * norm_step
    return (
        output,
        input_grad,
        norm_grad,
        norm_new,
        norm_first_new,
        norm_second_new,
        router_grad,
        router_new,
        router_first_new,
        router_second_new,
        block_grad[None],
        attend_master_new[None],
        attend_first_new[None],
        attend_second_new[None],
        expert_grad,
        expert_master_new,
        expert_first_new,
        expert_second_new,
        expert_average_new,
    )


def solution(mesh):
    return jax.shard_map(
        on_device,
        mesh=mesh,
        in_specs=(
            P("dp", "expert", None),
            P("dp", "expert", None),
            P(),
            P(),
            P(),
            P(),
            P(),
            P("expert", None, None, None),
            P("dp", "expert", None),
            P("dp", "expert", None),
            P(),
            P(),
            P("expert", None, None),
            P("expert", None, None),
            P("expert", None, None),
            P("expert", None, None),
            P("expert", None, None),
            P("expert", None, None, "dp"),
            P("expert", None, None, "dp"),
            P("expert", None, None, "dp"),
            P("expert", None, None, "dp"),
            P("expert", None, None),
            P(),
            P(),
            P(),
            P(),
        ),
        out_specs=(
            P("dp", "expert", None),
            P("dp", "expert", None),
            P(),
            P(),
            P(),
            P(),
            P(),
            P(),
            P(),
            P(),
            P("expert", None, None),
            P("expert", None, None),
            P("expert", None, None),
            P("expert", None, None),
            P("expert", None, None, "dp"),
            P("expert", None, None, "dp"),
            P("expert", None, None, "dp"),
            P("expert", None, None, "dp"),
            P("expert", None, None, "dp"),
        ),
        check_vma=False,
    )
```

profile of v0, /device:TPU:0, one launch (start us, length us, event | category | flops | bytes accessed | tf_op | source)
XLA Modules:
  0.0 733.5 jit_solution(1295930509613551395)
XLA Ops:
  0.7 7.6 %all-to-all-start = ((bf16[8,128,768]{2,1,0:T(8,128)(2,1)}), bf16[8,128,768]{2,1,0:T(8,128)(2,1)}, u32[]{:S(2)}, u32[]{:S(2)}) async-start(bf16[8,128,768]{2,1,0:T(8,128)(2,1)} %param.26), calls=%async_computation | async-start | bytes 3145728 | tf_op jit(solution)/shard_map/all_to_all | solution.py:486
  14.0 4.7 collective-permute-start
  19.3 2.9 collective-permute-start.3
  23.7 6.9 send_rows.3
  30.5 4.2 collective-permute-done
  35.3 10.2 %all-to-all-done = bf16[8,128,768]{2,1,0:T(8,128)(2,1)} async-done(((bf16[8,128,768]{2,1,0:T(8,128)(2,1)}), bf16[8,128,768]{2,1,0:T(8,128)(2,1)}, u32[]{:S(2)}, u32[]{:S(2)}) %all-to-all-start) | async-done | bytes 1572896 | tf_op jit(solution)/shard_map/all_to_all | solution.py:486
  45.5 4.5 all-to-all-start.1
  50.1 2.5 collective-permute-start.6
  58.1 59.7 %collective-permute-done.6 = s32[2,128]{1,0:T(2,128)S(1)} collective-permute-done((s32[2,128]{1,0:T(2,128)}, s32[2,128]{1,0:T(2,128)S(1)}, u32[]{:S(2)}, u32[]{:S(2)}) %collective-permute-start.6) | collective-permute-done | bytes 1056 | tf_op jit(solution)/shard_map/ppermute | solution.py:499
  130.4 2.0 fusion.15
  133.0 2.0 fusion.22
  135.1 5.5 convolution_convert_fusion.1.q_ref.k_ref.v_ref
  140.5 22.1 %attend.1 = (bf16[1024,768]{1,0:T(8,128)(2,1)}, f32[1024,768]{1,0:T(8,128)}) custom-call(s32[1]{0:T(128)} %bitcast.1.start_ref, bf16[1024,2304]{1,0:T(8,128)(2,1)} %convolution_convert_fusion.1.q_ref.k_ref.v_ref, bf16[1024,2304]{1,0:T(8,128)(2,1)} %convolution_convert_fusion.1.q_ref.k_ref.v_ref, bf16[1024,2304]{1,0:T(8,128)(2,1)} %convolution_convert_fusion.1.q_ref.k_ref.v_ref), custom_call_target="tpu_custom_call" | custom-call | flops 1610612736 | bytes 9437184 | tf_op jit(solution)/shard_map/attend/pallas_call | solution.py:165
  162.6 3.8 fusion.99
  168.8 6.9 send_rows.2
  175.7 22.3 %all-to-all-start.2 = ((bf16[8,8,40,768]{3,2,1,0:T(8,128)(2,1)}), bf16[8,8,40,768]{3,2,1,0:T(8,128)(2,1)}, u32[]{:S(2)}, u32[]{:S(2)}) async-start(bf16[8,8,40,768]{3,2,1,0:T(8,128)(2,1)} %send_rows.2), calls=%async_computation.2 | async-start | bytes 7864320 | tf_op jit(solution)/shard_map/all_to_all | solution.py:547
  198.8 2.7 convolution_bitcast_fusion.1
  208.1 2.4 copy.262
  210.5 1.9 copy-done.10
  212.4 17.5 %convolution_convert_fusion.u_ref = bf16[2560,3072]{1,0:T(8,128)(2,1)} fusion(bf16[2560,768]{1,0:T(8,128)(2,1)S(1)} %bitcast.237, bf16[1,2,768,3072]{3,2,1,0:T(8,128)(2,1)} %w_ref.1), kind=kOutput, calls=%fused_computation.1 | convolution fusion | flops 12087459840 | bytes 24379392 | tf_op jit(solution)/shard_map/dot_general | solution.py:595
  229.9 56.8 %all-to-all-done.2 = bf16[8,8,40,768]{3,2,1,0:T(8,128)(2,1)} async-done(((bf16[8,8,40,768]{3,2,1,0:T(8,128)(2,1)}), bf16[8,8,40,768]{3,2,1,0:T(8,128)(2,1)}, u32[]{:S(2)}, u32[]{:S(2)}) %all-to-all-start.2) | async-done | bytes 3932192 | tf_op jit(solution)/shard_map/all_to_all | solution.py:547
  286.7 4.3 all-to-all-start.3
  293.6 50.4 %expert_stage.1 = (bf16[2560,3072]{1,0:T(8,128)(2,1)}, bf16[2560,3072]{1,0:T(8,128)(2,1)}, bf16[2560,768]{1,0:T(8,128)(2,1)}, f32[2560,1]{1,0:T(8,128)}) custom-call(bf16[2560,768]{1,0:T(8,128)(2,1)} %bitcast.37.x_ref, bf16[2560,3072]{1,0:T(8,128)(2,1)} %convolution_convert_fusion.u_ref, bf16[1,2,768,3072]{3,2,1,0:T(8,128)(2,1)} %w_ref.1), custom_call_target="tpu_custom_call" | custom-call | flops 24159191040 | bytes 47185920 | tf_op jit(solution)/shard_map/expert_stage/pallas_call | solution.py:251
  344.1 2.3 reduce.7
  349.2 8.4 %trade.1 = f32[8,8,128]{2,1,0:T(8,128)} custom-call(f32[8,8,128]{2,1,0:T(8,128)} %bitcast.246), custom_call_target="tpu_custom_call" | custom-call | tf_op jit(solution)/shard_map/trade/pallas_call | solution.py:393
  358.9 5.7 all-to-all-start.4
  367.5 17.0 %multiply_convert_fusion.1 = bf16[768,3072]{1,0:T(8,128)(2,1)S(1)} fusion(bf16[2560,3072]{1,0:T(8,128)(2,1)} %get-tuple-element.59, f32[]{:T(128)S(6)} %convert_element_type.207, bf16[2560,768]{1,0:T(8,128)(2,1)} %bitcast.37.x_ref, f32[2560]{0:T(1024)} %mul.329), kind=kOutput, calls=%fused_computation.5 | convolution fusion | flops 12090212352 | bytes 24389636 | tf_op jit(solution)/shard_map/rd,rf->df/dot_general | solution.py:635
  387.9 18.1 %convolution_convert_fusion.3 = bf16[2560,768]{1,0:T(8,128)(2,1)} fusion(bf16[2560,3072]{1,0:T(8,128)(2,1)} %get-tuple-element.56, bf16[1,2,768,3072]{3,2,1,0:T(8,128)(2,1)} %w_ref.1), kind=kOutput, calls=%fused_computation.10 | convolution fusion | flops 12081561600 | bytes 24379392 | tf_op jit(solution)/shard_map/rf,df->rd/dot_general | solution.py:630
  406.0 18.0 %multiply_convert_fusion = bf16[768,3072]{1,0:T(8,128)(2,1)} fusion(bf16[2560,3072]{1,0:T(8,128)(2,1)} %get-tuple-element.56, f32[]{:T(128)S(6)} %convert_element_type.207, bf16[2560,768]{1,0:T(8,128)(2,1)S(1)} %bitcast.238, f32[2560]{0:T(1024)S(1)} %copy-done.54), kind=kOutput, calls=%fused_computation.4 | convolution fusion | flops 12090212352 | bytes 24389636 | tf_op jit(solution)/shard_map/rd,rf->df/dot_general | solution.py:636
  432.6 4.5 add_convert_fusion.6
  437.1 2.2 add_convert_fusion.4
  439.3 10.8 %all-to-all-done.4 = bf16[8,8,40,768]{3,2,1,0:T(8,128)(2,1)} async-done(((bf16[8,8,40,768]{3,2,1,0:T(8,128)(2,1)}), bf16[8,8,40,768]{3,2,1,0:T(8,128)(2,1)}, u32[]{:S(2)}, u32[]{:S(2)}) %all-to-all-start.4) | async-done | bytes 3932192 | tf_op jit(solution)/shard_map/all_to_all | solution.py:547
  450.1 5.1 all-to-all-start.5
  455.3 3.4 fusion.9
  458.7 4.6 multiply_reduce_fusion
  463.4 2.5 convert_add_fusion
  465.9 2.6 convolution_convert_fusion.4.g_ref
  468.5 38.3 %attend_back.1 = (bf16[1024,768]{1,0:T(8,128)(2,1)}, bf16[1024,768]{1,0:T(8,128)(2,1)}, bf16[1024,768]{1,0:T(8,128)(2,1)}) custom-call(s32[1]{0:T(128)} %bitcast.1.start_ref, bf16[1024,2304]{1,0:T(8,128)(2,1)} %convolution_convert_fusion.1.q_ref.k_ref.v_ref, bf16[1024,2304]{1,0:T(8,128)(2,1)} %convolution_convert_fusion.1.q_ref.k_ref.v_ref, ...), custom_call_target="tpu_custom_call" | custom-call | flops 4026531840 | bytes 15728640 | tf_op jit(solution)/shard_map/attend_back/pallas_call | solution.py:190
  510.2 8.2 %fusion.24 = (f32[1024]{0:T(1024)}, bf16[768]{0:T(1024)(128)(2,1)S(1)}, f32[1024]{0:T(1024)}, bf16[768]{0:T(1024)(128)(2,1)S(1)}, f32[1024,768]{1,0:T(8,128)}) fusion(bf16[8,128,768]{2,1,0:T(8,128)(2,1)} %all-to-all-done, f32[768]{0:T(1024)S(1)} %copy-done.33, f32[1024]{0:T(1024)S(1)} %copy-done.37, f32[1024]{0:T(1024)S(1)} %copy-done.35, ...), kind=kOutput, calls=%fused_computation.40 | convolution fusion | flops 3631739392 | bytes 12998656 | tf_op jit(solution)/shard_map/re,de->rd/dot_general | solution.py:687
  520.6 3.9 convolution_convert_fusion.5
  524.8 4.1 convolution_convert_fusion.2
  535.0 4.8 fusion.28
  539.8 21.7 %collective-permute-done.14.refs_1_ = bf16[768,768]{1,0:T(8,128)(2,1)} collective-permute-done((bf16[768,768]{1,0:T(8,128)(2,1)}, bf16[768,768]{1,0:T(8,128)(2,1)}, u32[]{:S(2)}, u32[]{:S(2)}) %collective-permute-start.14) | collective-permute-done | bytes 1179680 | tf_op jit(solution)/shard_map/ppermute | solution.py:513
  561.5 24.8 %collective-permute-done.15.refs_3_ = bf16[768,768]{1,0:T(8,128)(2,1)} collective-permute-done((bf16[768,768]{1,0:T(8,128)(2,1)}, bf16[768,768]{1,0:T(8,128)(2,1)}, u32[]{:S(2)}, u32[]{:S(2)}) %collective-permute-start.15) | collective-permute-done | bytes 1179680 | tf_op jit(solution)/shard_map/ppermute | solution.py:513
  586.3 6.0 all-to-all-start.6
  592.3 3.0 add_convert_fusion.2
  597.3 26.6 %collective-permute-done.13 = bf16[192,3200]{1,0:T(8,128)(2,1)} collective-permute-done((bf16[192,3200]{1,0:T(8,128)(2,1)}, bf16[192,3200]{1,0:T(8,128)(2,1)}, u32[]{:S(2)}, u32[]{:S(2)}) %collective-permute-start.13) | collective-permute-done | bytes 1228832 | tf_op jit(solution)/shard_map/ppermute | solution.py:513
  623.9 3.5 add_convert_fusion.1.block_ref.small_ref
  627.4 6.1 deal.1
  633.4 6.0 all-to-all-start.7
  639.5 2.7 copy.269
  642.1 2.4 copy.270.basis_ref
  644.5 21.5 %refresh.1 = (f32[1,2,768,768]{3,2,1,0:T(8,128)}, f32[1,2,768,768]{3,2,1,0:T(8,128)}, f32[1,2,768,768]{3,2,1,0:T(8,128)}, f32[1,2,768,768]{3,2,1,0:T(8,128)}, f32[1,2,768,768]{3,2,1,0:T(8,128)}) custom-call(s32[1]{0:T(128)} %bitcast.59.flag_ref, bf16[768,768]{1,0:T(8,128)(2,1)} %copy.270.basis_ref, bf16[768,768]{1,0:T(8,128)(2,1)} %bitcast.233, ...), custom_call_target="tpu_custom_call" | custom-call | flops 3623878656 | bytes 44826624 | tf_op jit(solution)/shard_map/refresh/pallas_call | solution.py:299
  666.0 9.1 %all-to-all-done.7 = bf16[8,192,512]{2,1,0:T(8,128)(2,1)} async-done(((bf16[8,192,512]{2,1,0:T(8,128)(2,1)}), bf16[8,192,512]{2,1,0:T(8,128)(2,1)}, u32[]{:S(2)}, u32[]{:S(2)}) %all-to-all-start.7) | async-done | bytes 1572896 | tf_op jit(solution)/shard_map/all_to_all | solution.py:547
  675.1 2.4 reduce_sum.242
  678.9 3.2 fusion.7
  685.7 4.5 all-to-all-start.8
  702.2 2.4 slice_bitcast_fusion
  704.5 4.7 fusion.30
  709.2 3.7 fusion.53
  712.9 6.2 fusion.29
  719.1 8.9 %all-to-all-done.8 = bf16[8,128,768]{2,1,0:T(8,128)(2,1)} async-done(((bf16[8,128,768]{2,1,0:T(8,128)(2,1)}), bf16[8,128,768]{2,1,0:T(8,128)(2,1)}, u32[]{:S(2)}, u32[]{:S(2)}) %all-to-all-start.8) | async-done | bytes 1572896 | tf_op jit(solution)/shard_map/all_to_all | solution.py:486
  728.0 2.7 copy.311
  730.7 2.7 copy.312
  (244 shorter events, 88.3 us)
Async XLA Ops:
  0.7 134.4 %copy-start = (bf16[768,2304]{1,0:T(8,128)(2,1)S(1)}, bf16[768,2304]{1,0:T(8,128)(2,1)}, u32[]{:S(2)}) copy-start(bf16[768,2304]{1,0:T(8,128)(2,1)} %param.28) | copy-start | bytes 10616836
  0.7 7.6 %copy-start.47 = (s32[8,128,2]{1,2,0:T(2,128)S(1)}, s32[8,128,2]{1,2,0:T(2,128)}, u32[]{:S(2)}) copy-start(s32[8,128,2]{1,2,0:T(2,128)} %param.34) | copy-start | bytes 24580
  0.7 44.8 %all-to-all-start = ((bf16[8,128,768]{2,1,0:T(8,128)(2,1)}), bf16[8,128,768]{2,1,0:T(8,128)(2,1)}, u32[]{:S(2)}, u32[]{:S(2)}) async-start(bf16[8,128,768]{2,1,0:T(8,128)(2,1)} %param.26), calls=%async_computation | async-start | bytes 3145728 | tf_op jit(solution)/shard_map/all_to_all | solution.py:486
  13.4 10.2 %copy-start.24 = (s32[8,128,2]{1,2,0:T(2,128)}, s32[8,128,2]{1,2,0:T(2,128)S(1)}, u32[]{:S(2)}) copy-start(s32[8,128,2]{1,2,0:T(2,128)S(1)} %compare_select_fusion.1) | copy-start | bytes 24580
  14.0 20.7 %collective-permute-start = (s32[2,128]{1,0:T(2,128)}, s32[2,128]{1,0:T(2,128)S(1)}, u32[]{:S(2)}, u32[]{:S(2)}) collective-permute-start(s32[2,128]{1,0:T(2,128)} %get-tuple-element.256), channel_id=1, source_target_pairs={{0,7},{1,0},{2,1},{3,2},{4,3},{5,4},{6,5},{7,6},{8,15},{9,8},{10,9... | collective-permute-start | bytes 3080 | tf_op jit(solution)/shard_map/ppermute | solution.py:499
  18.8 31.3 %collective-permute-start.1 = (s32[2,128]{1,0:T(2,128)}, s32[2,128]{1,0:T(2,128)}, u32[]{:S(2)}, u32[]{:S(2)}) collective-permute-start(s32[2,128]{1,0:T(2,128)} %get-tuple-element.255), channel_id=1, source_target_pairs={{0,6},{1,7},{2,0},{3,1},{4,2},{5,3},{6,4},{7,5},{8,14},{9,15},{10,... | collective-permute-start | bytes 3080 | tf_op jit(solution)/shard_map/ppermute | solution.py:499
  19.3 34.5 %collective-permute-start.2 = (s32[2,128]{1,0:T(2,128)}, s32[2,128]{1,0:T(2,128)}, u32[]{:S(2)}, u32[]{:S(2)}) collective-permute-start(s32[2,128]{1,0:T(2,128)} %get-tuple-element.254), channel_id=1, source_target_pairs={{0,5},{1,6},{2,7},{3,0},{4,1},{5,2},{6,3},{7,4},{8,13},{9,14},{10,... | collective-permute-start | bytes 3080 | tf_op jit(solution)/shard_map/ppermute | solution.py:499
  19.3 35.7 %collective-permute-start.3 = (s32[2,128]{1,0:T(2,128)}, s32[2,128]{1,0:T(2,128)}, u32[]{:S(2)}, u32[]{:S(2)}) collective-permute-start(s32[2,128]{1,0:T(2,128)} %get-tuple-element.253), channel_id=1, source_target_pairs={{0,4},{1,5},{2,6},{3,7},{4,0},{5,1},{6,2},{7,3},{8,12},{9,13},{10,... | collective-permute-start | bytes 3080 | tf_op jit(solution)/shard_map/ppermute | solution.py:499
  22.3 34.0 %collective-permute-start.4 = (s32[2,128]{1,0:T(2,128)}, s32[2,128]{1,0:T(2,128)}, u32[]{:S(2)}, u32[]{:S(2)}) collective-permute-start(s32[2,128]{1,0:T(2,128)} %get-tuple-element.252), channel_id=1, source_target_pairs={{0,3},{1,4},{2,5},{3,6},{4,7},{5,0},{6,1},{7,2},{8,11},{9,12},{10,... | collective-permute-start | bytes 3080 | tf_op jit(solution)/shard_map/ppermute | solution.py:499
  34.7 22.8 %collective-permute-start.5 = (s32[2,128]{1,0:T(2,128)}, s32[2,128]{1,0:T(2,128)S(1)}, u32[]{:S(2)}, u32[]{:S(2)}) collective-permute-start(s32[2,128]{1,0:T(2,128)} %get-tuple-element.251), channel_id=1, source_target_pairs={{0,2},{1,3},{2,4},{3,5},{4,6},{5,7},{6,0},{7,1},{8,10},{9,11},{10,... | collective-permute-start | bytes 3080 | tf_op jit(solution)/shard_map/ppermute | solution.py:499
  45.5 130.1 %all-to-all-start.1 = ((bf16[8,8,40,768]{3,2,1,0:T(8,128)(2,1)}), bf16[8,8,40,768]{3,2,1,0:T(8,128)(2,1)}, u32[]{:S(2)}, u32[]{:S(2)}) async-start(bf16[8,8,40,768]{3,2,1,0:T(8,128)(2,1)} %send_rows.3), calls=%async_computation.1 | async-start | bytes 7864320 | tf_op jit(solution)/shard_map/all_to_all | solution.py:547
  50.0 83.0 %copy-start.32 = (f32[768]{0:T(1024)S(1)}, f32[768]{0:T(1024)}, u32[]{:S(2)}) copy-start(f32[768]{0:T(1024)} %get-tuple-element.265) | copy-start | bytes 9220
  50.1 83.0 %copy-start.49 = (f32[768]{0:T(1024)S(1)}, f32[768]{0:T(1024)}, u32[]{:S(2)}) copy-start(f32[768]{0:T(1024)} %get-tuple-element.223) | copy-start | bytes 9220
  50.1 67.7 %collective-permute-start.6 = (s32[2,128]{1,0:T(2,128)}, s32[2,128]{1,0:T(2,128)S(1)}, u32[]{:S(2)}, u32[]{:S(2)}) collective-permute-start(s32[2,128]{1,0:T(2,128)} %get-tuple-element.250), channel_id=1, source_target_pairs={{0,1},{1,2},{2,3},{3,4},{4,5},{5,6},{6,7},{7,0},{8,9},{9,10},{10,1... | collective-permute-start | bytes 3080 | tf_op jit(solution)/shard_map/ppermute | solution.py:499
  128.7 72.8 %copy-start.25 = (s32[8,2,128]{2,1,0:T(2,128)}, s32[8,2,128]{2,1,0:T(2,128)S(1)}, u32[]{:S(2)}) copy-start(s32[8,2,128]{2,1,0:T(2,128)S(1)} %get-tuple-element.230) | copy-start | bytes 24580
  135.1 5.5 copy-start.13
  175.7 111.0 %all-to-all-start.2 = ((bf16[8,8,40,768]{3,2,1,0:T(8,128)(2,1)}), bf16[8,8,40,768]{3,2,1,0:T(8,128)(2,1)}, u32[]{:S(2)}, u32[]{:S(2)}) async-start(bf16[8,8,40,768]{3,2,1,0:T(8,128)(2,1)} %send_rows.2), calls=%async_computation.2 | async-start | bytes 7864320 | tf_op jit(solution)/shard_map/all_to_all | solution.py:547
  198.8 3.9 copy-start.38
  198.8 4.4 copy-start.42
  286.7 72.3 %all-to-all-start.3 = ((bf16[8,128,768]{2,1,0:T(8,128)(2,1)}), bf16[8,128,768]{2,1,0:T(8,128)(2,1)}, u32[]{:S(2)}, u32[]{:S(2)}) async-start(bf16[8,128,768]{2,1,0:T(8,128)(2,1)} %param.27), calls=%async_computation.3 | async-start | bytes 3145728 | tf_op jit(solution)/shard_map/all_to_all | solution.py:486
  358.9 91.2 %all-to-all-start.4 = ((bf16[8,8,40,768]{3,2,1,0:T(8,128)(2,1)}), bf16[8,8,40,768]{3,2,1,0:T(8,128)(2,1)}, u32[]{:S(2)}, u32[]{:S(2)}) async-start(bf16[8,8,40,768]{3,2,1,0:T(8,128)(2,1)} %bitcast.240), calls=%async_computation.4 | async-start | bytes 7864320 | tf_op jit(solution)/shard_map/all_to_all | solution.py:547
  384.5 2.9 copy-start.8
  387.4 45.2 %collective-permute-start.8 = (bf16[768,768]{1,0:T(8,128)(2,1)}, bf16[768,768]{1,0:T(8,128)(2,1)}, u32[]{:S(2)}, u32[]{:S(2)}) collective-permute-start(bf16[768,768]{1,0:T(8,128)(2,1)} %get-tuple-element.240), channel_id=1, source_target_pairs={{0,8},{8,0},{16,24},{24,16},{1,9},{9,1},{17,25},{25,17},{2,10},{10... | collective-permute-start | bytes 3538952 | tf_op jit(solution)/shard_map/ppermute | solution.py:516
  387.4 18.6 %copy-start.11 = (bf16[1,8,8,40,768]{4,3,2,1,0:T(8,128)(2,1)S(1)}, bf16[1,8,8,40,768]{4,3,2,1,0:T(8,128)(2,1)}, u32[]{:S(2)}) copy-start(bf16[1,8,8,40,768]{4,3,2,1,0:T(8,128)(2,1)} %copy-done.10) | copy-start | bytes 11796484
  387.4 18.6 %copy-start.54 = (f32[2560]{0:T(1024)S(1)}, f32[2560]{0:T(1024)}, u32[]{:S(2)}) copy-start(f32[2560]{0:T(1024)} %mul.329) | copy-start | bytes 30724
  387.4 45.2 %collective-permute-start.7 = (bf16[768,768]{1,0:T(8,128)(2,1)}, bf16[768,768]{1,0:T(8,128)(2,1)}, u32[]{:S(2)}, u32[]{:S(2)}) collective-permute-start(bf16[768,768]{1,0:T(8,128)(2,1)} %get-tuple-element.241), channel_id=1, source_target_pairs={{0,8},{8,0},{16,24},{24,16},{1,9},{9,1},{17,25},{25,17},{2,10},{10... | collective-permute-start | bytes 3538952 | tf_op jit(solution)/shard_map/ppermute | solution.py:516
  428.2 3.0 copy-start.46
  428.2 3.0 copy-start.26
  428.2 3.0 copy-start.4
  430.1 6.9 collective-permute-start.10
  430.2 6.9 collective-permute-start.9
  432.6 4.5 copy-start.9
  450.1 5.1 copy-start.40
  450.1 136.2 %all-to-all-start.5 = ((bf16[8,8,40,768]{3,2,1,0:T(8,128)(2,1)}), bf16[8,8,40,768]{3,2,1,0:T(8,128)(2,1)}, u32[]{:S(2)}, u32[]{:S(2)}) async-start(bf16[8,8,40,768]{3,2,1,0:T(8,128)(2,1)} %bitcast.239), calls=%async_computation.5 | async-start | bytes 7864320 | tf_op jit(solution)/shard_map/all_to_all | solution.py:547
  455.2 3.4 copy-start.2
  455.2 3.4 copy-start.22
  455.3 3.4 copy-start.23
  455.3 3.4 copy-start.28
  510.1 8.2 %copy-start.19 = (bf16[1024,2304]{1,0:T(8,128)(2,1)}, bf16[1024,2304]{1,0:T(8,128)(2,1)S(1)}, u32[]{:S(2)}) copy-start(bf16[1024,2304]{1,0:T(8,128)(2,1)S(1)} %constant_dynamic-update-slice_fusion.16) | copy-start | bytes 14155780
  510.1 8.2 %copy-start.55 = (bf16[768]{0:T(1024)(128)(2,1)S(1)}, bf16[768]{0:T(1024)(128)(2,1)}, u32[]{:S(2)}) copy-start(bf16[768]{0:T(1024)(128)(2,1)} %get-tuple-element.210) | copy-start | bytes 4612
  510.1 8.3 %copy-start.29 = (bf16[768,8]{0,1:T(8,128)(2,1)S(1)}, bf16[768,8]{0,1:T(8,128)(2,1)}, u32[]{:S(2)}) copy-start(bf16[768,8]{0,1:T(8,128)(2,1)} %convolution_convert_fusion.8) | copy-start | bytes 36868
  520.6 4.0 copy-start.14
  520.6 4.2 copy-start.20
  524.8 4.1 copy-start.18
  529.3 3.0 copy-start.5
  529.4 5.7 copy-start.56
  532.3 60.0 %collective-permute-start.12 = (bf16[192,3200]{1,0:T(8,128)(2,1)}, bf16[192,3200]{1,0:T(8,128)(2,1)}, u32[]{:S(2)}, u32[]{:S(2)}) collective-permute-start(bf16[192,3200]{1,0:T(8,128)(2,1)} %get-tuple-element.233), channel_id=1, source_target_pairs={{0,8},{8,0},{16,24},{24,16},{1,9},{9,1},{17,25},{25,17},{2,10},{10... | collective-permute-start | bytes 3686408 | tf_op jit(solution)/shard_map/ppermute | solution.py:516
  532.3 29.2 %collective-permute-start.14 = (bf16[768,768]{1,0:T(8,128)(2,1)}, bf16[768,768]{1,0:T(8,128)(2,1)}, u32[]{:S(2)}, u32[]{:S(2)}) collective-permute-start(bf16[768,768]{1,0:T(8,128)(2,1)} %get-tuple-element.236), channel_id=1, source_target_pairs={{0,16},{8,24},{16,0},{24,8},{1,17},{9,25},{17,1},{25,9},{2,18},{10... | collective-permute-start | bytes 3538952 | tf_op jit(solution)/shard_map/ppermute | solution.py:513
  533.7 52.6 %collective-permute-start.15 = (bf16[768,768]{1,0:T(8,128)(2,1)}, bf16[768,768]{1,0:T(8,128)(2,1)}, u32[]{:S(2)}, u32[]{:S(2)}) collective-permute-start(bf16[768,768]{1,0:T(8,128)(2,1)} %get-tuple-element.234), channel_id=1, source_target_pairs={{0,16},{8,24},{16,0},{24,8},{1,17},{9,25},{17,1},{25,9},{2,18},{10... | collective-permute-start | bytes 3538952 | tf_op jit(solution)/shard_map/ppermute | solution.py:513
  534.3 63.0 %collective-permute-start.11 = (bf16[192,3200]{1,0:T(8,128)(2,1)}, bf16[192,3200]{1,0:T(8,128)(2,1)}, u32[]{:S(2)}, u32[]{:S(2)}) collective-permute-start(bf16[192,3200]{1,0:T(8,128)(2,1)} %get-tuple-element.232), channel_id=1, source_target_pairs={{0,8},{8,0},{16,24},{24,16},{1,9},{9,1},{17,25},{25,17},{2,10},{10... | collective-permute-start | bytes 3686408 | tf_op jit(solution)/shard_map/ppermute | solution.py:516
  586.3 47.1 %all-to-all-start.6 = ((bf16[8,128,768]{2,1,0:T(8,128)(2,1)}), bf16[8,128,768]{2,1,0:T(8,128)(2,1)}, u32[]{:S(2)}, u32[]{:S(2)}) async-start(bf16[8,128,768]{2,1,0:T(8,128)(2,1)} %bitcast.235), calls=%async_computation.6 | async-start | bytes 3145728 | tf_op jit(solution)/shard_map/all_to_all | solution.py:486
  592.3 4.4 copy-start.58
  595.2 28.6 %collective-permute-start.13 = (bf16[192,3200]{1,0:T(8,128)(2,1)}, bf16[192,3200]{1,0:T(8,128)(2,1)}, u32[]{:S(2)}, u32[]{:S(2)}) collective-permute-start(bf16[192,3200]{1,0:T(8,128)(2,1)} %add_convert_fusion.2), channel_id=1, source_target_pairs={{0,16},{8,24},{16,0},{24,8},{1,17},{9,25},{17,1},{25,9},{2,18},{10... | collective-permute-start | bytes 3686408 | tf_op jit(solution)/shard_map/ppermute | solution.py:513
  633.4 41.6 %all-to-all-start.7 = ((bf16[8,192,512]{2,1,0:T(8,128)(2,1)}), bf16[8,192,512]{2,1,0:T(8,128)(2,1)}, u32[]{:S(2)}, u32[]{:S(2)}) async-start(bf16[8,192,512]{2,1,0:T(8,128)(2,1)} %deal.1), calls=%async_computation.7 | async-start | bytes 3145728 | tf_op jit(solution)/shard_map/all_to_all | solution.py:547
  644.5 34.3 %copy-start.41 = (s32[8,1,128]{2,1,0:T(1,128)S(1)}, s32[8,1,128]{2,1,0:T(1,128)}, u32[]{:S(2)}) copy-start(s32[8,1,128]{2,1,0:T(1,128)} %copy-done.38) | copy-start | bytes 12292
  644.5 34.3 %copy-start.44 = (s32[8,1,128]{2,1,0:T(1,128)S(1)}, s32[8,1,128]{2,1,0:T(1,128)}, u32[]{:S(2)}) copy-start(s32[8,1,128]{2,1,0:T(1,128)} %copy-done.42) | copy-start | bytes 12292
  644.5 34.3 %copy-start.51 = (f32[8,1,128]{2,1,0:T(1,128)S(1)}, f32[8,1,128]{2,1,0:T(1,128)}, u32[]{:S(2)}) copy-start(f32[8,1,128]{2,1,0:T(1,128)} %copy-done.50) | copy-start | bytes 12292
  644.5 34.3 %copy-start.53 = (f32[8,1,128]{2,1,0:T(1,128)S(1)}, f32[8,1,128]{2,1,0:T(1,128)}, u32[]{:S(2)}) copy-start(f32[8,1,128]{2,1,0:T(1,128)} %copy-done.52) | copy-start | bytes 12292
  677.4 5.9 copy-start.12
  677.4 6.7 copy-start.3
  677.4 5.9 collective-permute-start.16
  684.1 7.1 collective-permute-start.17
  685.7 42.3 %all-to-all-start.8 = ((bf16[8,128,768]{2,1,0:T(8,128)(2,1)}), bf16[8,128,768]{2,1,0:T(8,128)(2,1)}, u32[]{:S(2)}, u32[]{:S(2)}) async-start(bf16[8,128,768]{2,1,0:T(8,128)(2,1)} %bitcast.236), calls=%async_computation.8 | async-start | bytes 3145728 | tf_op jit(solution)/shard_map/all_to_all | solution.py:486
  697.6 11.6 %copy-start.30 = (f32[768,4]{0,1:T(4,128)}, f32[768,4]{0,1:T(4,128)S(1)}, u32[]{:S(2)}) copy-start(f32[768,4]{0,1:T(4,128)S(1)} %copy.276) | copy-start | bytes 36868
  (22 other events, 35.9 us)
where the time goes:
time: 745 us; the launch traced here: 734 us
  waiting for transfers between devices  234 us (31%)
  Pallas kernels  160 us (21%)
  matrix products  125 us (17%)
  starting transfers between devices  82.7 us (11%)
  local copies, waits for them, and re-layouts  77.3 us (10%)
  other arithmetic  51.5 us (7%)
    all_to_all x5, waiting for transfers between devices, exchange(): lax.all_to_all(value, 'expert', split_axis=0, concat_axis=0, tiled=True)  76.6 us
    ppermute x4, waiting for transfers between devices, dp_move(): lax.ppermute(value, 'dp', [(d, (d + 2 * shift) % dp_count) for d in range...  74.2 us
    ppermute x7, waiting for transfers between devices, ring(): rows.append(lax.ppermute(given, 'expert', moves))  63.9 us
    pallas_call x1, Pallas kernels, expert_stage(): pl.pallas_call(expert_kernel, grid=(rows // TILE,), out_shape=(jax.ShapeD...  50.4 us
    all_to_all x5, starting transfers between devices, exchange(): lax.all_to_all(value, 'expert', split_axis=0, concat_axis=0, tiled=True)  43.6 us
    pallas_call x1, Pallas kernels, attend_back(): pl.pallas_call(functools.partial(attend_back_kernel, whole), grid=(pairs,...  38.3 us
    unnamed x143, local copies, waits for them, and re-layouts  36.6 us
    all_to_all x4, starting transfers between devices, swap(): lax.all_to_all(value, 'expert', split_axis=0, concat_axis=0, tiled=True,...  22.4 us
  transfers between devices with their start and end apart: 27, of which 11 were waited for; matrix products, arithmetic and copies ran while one was open for 32% of the time, Pallas kernels for 22%

commit v1 on v0

--- a/solution.py
+++ b/solution.py
@@ -238,7 +238,7 @@
         gate_grad = here if gate_grad is None else gate_grad + here
         inputs = add if inputs is None else inputs + add
     input_ref[...] = inputs.astype(low)
-    gate_grad_ref[...] = gate_grad
+    gate_grad_ref[0] = gate_grad.T
 
 
 def expert_stage(x, u, w):
@@ -255,14 +255,19 @@
             jax.ShapeDtypeStruct((rows, hidden), low),
             jax.ShapeDtypeStruct((rows, hidden), low),
             jax.ShapeDtypeStruct((rows, width), low),
-            jax.ShapeDtypeStruct((rows, 1), wide),
+            jax.ShapeDtypeStruct((rows // TILE, 1, TILE), wide),
         ),
         in_specs=[
             row_block(width),
             row_block(hidden),
             pl.BlockSpec((1, 1, width, hidden), lambda i: (0, 0, 0, 0)),
         ],
-        out_specs=(row_block(hidden), row_block(hidden), row_block(width), row_block(1)),
+        out_specs=(
+            row_block(hidden),
+            row_block(hidden),
+            row_block(width),
+            pl.BlockSpec((1, 1, TILE), lambda i: (i, 0, 0)),
+        ),
         cost_estimate=pl.CostEstimate(
             flops=4 * rows * width * hidden,
             bytes_accessed=6 * rows * hidden,
@@ -320,23 +325,21 @@
 
 
 def deal_kernel(which_ref, block_ref, small_ref, out_ref):
-    width = block_ref.shape[1]
-    out_ref[0, :, :width] = block_ref[...]
-    out_ref[0, :, width:] = small_ref[...]
-
-
-def deal(which, rows, block_width, count):
-    height, total = rows.shape
-    extra = total - block_width * count
+    height = block_ref.shape[0]
+    out_ref[0, :height] = block_ref[...]
+    out_ref[0, height:] = small_ref[...]
+
+
+def deal(which, rows, small, count):
+    height, extra, block_width = rows.shape[0], small.shape[0], small.shape[1]
     if block_width % 128:
         return jnp.stack(
             [
                 jnp.concatenate(
                     [
                         lax.dynamic_slice_in_dim(rows, which[s] * block_width, block_width, 1),
-                        rows[:, total - extra :],
-                    ],
-                    axis=1,
+                        small,
+                    ]
                 )
                 for s in range(count)
             ]
@@ -348,13 +351,13 @@
             grid=(count,),
             in_specs=[
                 pl.BlockSpec((height, block_width), lambda s, which: (0, which[s])),
-                pl.BlockSpec((height, extra), lambda s, which: (0, total // extra - 1)),
+                pl.BlockSpec((extra, block_width), lambda s, which: (0, 0)),
             ],
-            out_specs=pl.BlockSpec((1, height, block_width + extra), lambda s, which: (s, 0, 0)),
-        ),
-        out_shape=jax.ShapeDtypeStruct((count, height, block_width + extra), rows.dtype),
+            out_specs=pl.BlockSpec((1, height + extra, block_width), lambda s, which: (s, 0, 0)),
+        ),
+        out_shape=jax.ShapeDtypeStruct((count, height + extra, block_width), rows.dtype),
         name="deal",
-    )(which, rows, rows)
+    )(which, rows, small)
 
 
 def trade_kernel(count, in_ref, out_ref, landed, send_sem, recv_sem):
@@ -534,14 +537,17 @@
         return [half[0]] + [dp_move(half[shift], shift) for shift in range(1, lines)]
 
     def gather_dp(value):
-        rows = jnp.stack([value] + [dp_move(value, shift) for shift in range(1, lines)])
-        others = other_core(rows)
-        out = jnp.zeros((dp_count,) + value.shape, value.dtype)
-        for shift in range(lines):
-            first = (line + lines - shift) % lines * 2
-            out = lax.dynamic_update_index_in_dim(out, rows[shift], first + core, 0)
-            out = lax.dynamic_update_index_in_dim(out, others[shift], first + 1 - core, 0)
-        return out.reshape((-1,) + value.shape[1:])
+        rows = [value] + [dp_move(value, shift) for shift in range(1, lines)]
+        others = [other_core(row) for row in rows]
+        pieces = []
+        for place in range(dp_count):
+            piece = None
+            for mine, theirs, shift in zip(rows, others, range(lines)):
+                here = jnp.where(core == place % 2, mine, theirs)
+                here = jnp.where((line + lines - shift) % lines == place // 2, here, 0)
+                piece = here if piece is None else piece + here
+            pieces.append(piece)
+        return pieces
 
     def exchange(value):
         return lax.all_to_all(value, "expert", split_axis=0, concat_axis=0, tiled=True)
@@ -714,15 +720,22 @@
     )
     half_rows = halve(grad_full, 0, cut_dp(grad_full, 0, 1 - core))
     my_rows = sum(term.astype(wide) for term in spread(half_rows)).astype(low)
-    my_rows = deal(which_block, my_rows, block_width, expert_count)
-    my_rows = after(exchange(after(my_rows, input_grad)), expert_grad)
+    height = my_rows.shape[0]
+    small_rows = -(-small_width // 16) * 16
+    small = jnp.pad(
+        my_rows[:, block_width * expert_count :][:, :small_width].T,
+        ((0, small_rows - small_width), (0, block_width - height)),
+    )
+    my_rows = deal(which_block, my_rows, small, expert_count)
+    my_rows = after(exchange(after(my_rows, input_grad, output_seq)), expert_grad)
     my_rows_done = my_rows
-    my_rows = jnp.sum(my_rows.astype(wide), axis=0)
-    summed = gather_dp(my_rows.astype(low)).astype(wide)
-    block_grad = summed[:, :block_width]
-    small_sum = summed[:, block_width : block_width + small_width]
-    router_grad = small_sum[:, :expert_total]
-    norm_grad = small_sum[:, expert_total:].T
+    pieces = gather_dp(jnp.sum(my_rows.astype(wide), axis=0).astype(low))
+    block_grad = jnp.concatenate([piece[:height] for piece in pieces]).astype(wide)
+    small_sum = jnp.concatenate(
+        [piece[height : height + small_width, :height] for piece in pieces], axis=1
+    ).astype(wide)
+    router_grad = small_sum[:expert_total].T
+    norm_grad = small_sum[expert_total:]
 
     left_basis = attend_left[0].astype(low)
     right_basis = attend_right[0].astype(low)

time: 745 us -> 738 us (level)
  waiting for transfers between devices: 234 us -> 223 us
    ppermute x4, waiting for transfers between devices: 74.2 us -> 60.2 us  [dp_move(): lax.ppermute(value, 'dp', [(d, (d + 2 * shift) % dp_count) for d in range...]
    all_to_all x4, waiting for transfers between devices: 19.2 us -> 26.9 us  [swap(): lax.all_to_all(value, 'expert', split_axis=0, concat_axis=0, tiled=True,...]
    unnamed x143 -> x149, local copies, waits for them, and re-layouts: 36.6 us -> 33.7 us
  transfers between devices with their start and end apart: 27 -> 28, of which waited for: 11 -> 12; matrix products, arithmetic and copies ran while one was open for 32% -> 33% of each run, Pallas kernels for 22% -> 22%
where the time goes in v1:
time: 738 us; the launch traced here: 727 us
  waiting for transfers between devices  223 us (30%)
  Pallas kernels  161 us (22%)
  matrix products  125 us (17%)
  starting transfers between devices  82.7 us (11%)
  local copies, waits for them, and re-layouts  79.9 us (11%)
  other arithmetic  52.8 us (7%)
    all_to_all x5, waiting for transfers between devices, exchange(): lax.all_to_all(value, 'expert', split_axis=0, concat_axis=0, tiled=True)  71.5 us
    ppermute x7, waiting for transfers between devices, ring(): rows.append(lax.ppermute(given, 'expert', moves))  63.9 us
    ppermute x4, waiting for transfers between devices, dp_move(): lax.ppermute(value, 'dp', [(d, (d + 2 * shift) % dp_count) for d in range...  60.2 us
    pallas_call x1, Pallas kernels, expert_stage(): pl.pallas_call(expert_kernel, grid=(rows // TILE,), out_shape=(jax.ShapeD...  50.4 us
    all_to_all x5, starting transfers between devices, exchange(): lax.all_to_all(value, 'expert', split_axis=0, concat_axis=0, tiled=True)  43.8 us
    pallas_call x1, Pallas kernels, attend_back(): pl.pallas_call(functools.partial(attend_back_kernel, whole), grid=(pairs,...  38.6 us
    unnamed x149, local copies, waits for them, and re-layouts  33.7 us
    all_to_all x4, waiting for transfers between devices, swap(): lax.all_to_all(value, 'expert', split_axis=0, concat_axis=0, tiled=True,...  26.9 us
  transfers between devices with their start and end apart: 28, of which 12 were waited for; matrix products, arithmetic and copies ran while one was open for 33% of the time, Pallas kernels for 22%

profile of v1, /device:TPU:0, one launch (start us, length us, event | category | flops | bytes accessed | tf_op | source)
XLA Modules:
  0.0 726.8 jit_solution(4663529995837612746)
XLA Ops:
  0.7 7.6 %all-to-all-start = ((bf16[8,128,768]{2,1,0:T(8,128)(2,1)}), bf16[8,128,768]{2,1,0:T(8,128)(2,1)}, u32[]{:S(2)}, u32[]{:S(2)}) async-start(bf16[8,128,768]{2,1,0:T(8,128)(2,1)} %param.26), calls=%async_computation | async-start | bytes 3145728 | tf_op jit(solution)/shard_map/all_to_all | solution.py:489
  14.0 4.7 collective-permute-start
  19.3 2.9 collective-permute-start.3
  23.7 6.9 send_rows.3
  30.5 4.2 collective-permute-done
  35.3 10.2 %all-to-all-done = bf16[8,128,768]{2,1,0:T(8,128)(2,1)} async-done(((bf16[8,128,768]{2,1,0:T(8,128)(2,1)}), bf16[8,128,768]{2,1,0:T(8,128)(2,1)}, u32[]{:S(2)}, u32[]{:S(2)}) %all-to-all-start) | async-done | bytes 1572896 | tf_op jit(solution)/shard_map/all_to_all | solution.py:489
  45.5 4.5 all-to-all-start.1
  50.1 2.5 collective-permute-start.6
  58.1 59.7 %collective-permute-done.6 = s32[2,128]{1,0:T(2,128)S(1)} collective-permute-done((s32[2,128]{1,0:T(2,128)}, s32[2,128]{1,0:T(2,128)S(1)}, u32[]{:S(2)}, u32[]{:S(2)}) %collective-permute-start.6) | collective-permute-done | bytes 1056 | tf_op jit(solution)/shard_map/ppermute | solution.py:502
  135.1 5.5 convolution_convert_fusion.1.q_ref.k_ref.v_ref
  140.5 22.1 %attend.1 = (bf16[1024,768]{1,0:T(8,128)(2,1)}, f32[1024,768]{1,0:T(8,128)}) custom-call(s32[1]{0:T(128)} %bitcast.1.start_ref, bf16[1024,2304]{1,0:T(8,128)(2,1)} %convolution_convert_fusion.1.q_ref.k_ref.v_ref, bf16[1024,2304]{1,0:T(8,128)(2,1)} %convolution_convert_fusion.1.q_ref.k_ref.v_ref, bf16[1024,2304]{1,0:T(8,128)(2,1)} %convolution_convert_fusion.1.q_ref.k_ref.v_ref), custom_call_target="tpu_custom_call" | custom-call | flops 1610612736 | bytes 9437184 | tf_op jit(solution)/shard_map/attend/pallas_call | solution.py:165
  162.6 3.8 fusion.115
  168.8 6.9 send_rows.2
  175.7 22.2 %all-to-all-start.2 = ((bf16[8,8,40,768]{3,2,1,0:T(8,128)(2,1)}), bf16[8,8,40,768]{3,2,1,0:T(8,128)(2,1)}, u32[]{:S(2)}, u32[]{:S(2)}) async-start(bf16[8,8,40,768]{3,2,1,0:T(8,128)(2,1)} %send_rows.2), calls=%async_computation.2 | async-start | bytes 7864320 | tf_op jit(solution)/shard_map/all_to_all | solution.py:553
  198.7 2.7 convolution_bitcast_fusion.1
  207.9 2.4 copy.181
  212.2 17.5 %convolution_convert_fusion.u_ref = bf16[2560,3072]{1,0:T(8,128)(2,1)} fusion(bf16[2560,768]{1,0:T(8,128)(2,1)S(1)} %bitcast.240, bf16[1,2,768,3072]{3,2,1,0:T(8,128)(2,1)} %w_ref.1), kind=kOutput, calls=%fused_computation.1 | convolution fusion | flops 12087459840 | bytes 24379392 | tf_op jit(solution)/shard_map/dot_general | solution.py:601
  229.7 56.7 %all-to-all-done.2 = bf16[8,8,40,768]{3,2,1,0:T(8,128)(2,1)} async-done(((bf16[8,8,40,768]{3,2,1,0:T(8,128)(2,1)}), bf16[8,8,40,768]{3,2,1,0:T(8,128)(2,1)}, u32[]{:S(2)}, u32[]{:S(2)}) %all-to-all-start.2) | async-done | bytes 3932192 | tf_op jit(solution)/shard_map/all_to_all | solution.py:553
  286.5 4.3 all-to-all-start.3
  293.5 50.4 %expert_stage.1 = (bf16[2560,3072]{1,0:T(8,128)(2,1)}, bf16[2560,3072]{1,0:T(8,128)(2,1)}, bf16[2560,768]{1,0:T(8,128)(2,1)}, f32[10,1,256]{2,1,0:T(1,128)}) custom-call(bf16[2560,768]{1,0:T(8,128)(2,1)} %bitcast.37.x_ref, bf16[2560,3072]{1,0:T(8,128)(2,1)} %convolution_convert_fusion.u_ref, bf16[1,2,768,3072]{3,2,1,0:T(8,128)(2,1)} %w_ref.1), custom_call_target="tpu_custom_call" | custom-call | flops 24159191040 | bytes 47185920 | tf_op jit(solution)/shard_map/expert_stage/pallas_call | solution.py:251
  348.1 8.4 %trade.1 = f32[8,8,128]{2,1,0:T(8,128)} custom-call(f32[8,8,128]{2,1,0:T(8,128)} %bitcast.246), custom_call_target="tpu_custom_call" | custom-call | tf_op jit(solution)/shard_map/trade/pallas_call | solution.py:396
  357.8 6.0 all-to-all-start.4
  366.7 17.0 %multiply_convert_fusion.1 = bf16[768,3072]{1,0:T(8,128)(2,1)S(1)} fusion(bf16[2560,3072]{1,0:T(8,128)(2,1)} %get-tuple-element.59, f32[]{:T(128)S(6)} %convert_element_type.223, bf16[2560,768]{1,0:T(8,128)(2,1)} %bitcast.37.x_ref, f32[2560]{0:T(1024)} %mul.325), kind=kOutput, calls=%fused_computation.5 | convolution fusion | flops 12090212352 | bytes 24389636 | tf_op jit(solution)/shard_map/rd,rf->df/dot_general | solution.py:641
  387.1 18.1 %convolution_convert_fusion.3 = bf16[2560,768]{1,0:T(8,128)(2,1)} fusion(bf16[2560,3072]{1,0:T(8,128)(2,1)} %get-tuple-element.56, bf16[1,2,768,3072]{3,2,1,0:T(8,128)(2,1)} %w_ref.1), kind=kOutput, calls=%fused_computation.10 | convolution fusion | flops 12081561600 | bytes 24379392 | tf_op jit(solution)/shard_map/rf,df->rd/dot_general | solution.py:636
  405.2 18.0 %multiply_convert_fusion = bf16[768,3072]{1,0:T(8,128)(2,1)} fusion(bf16[2560,3072]{1,0:T(8,128)(2,1)} %get-tuple-element.56, f32[]{:T(128)S(6)} %convert_element_type.223, bf16[2560,768]{1,0:T(8,128)(2,1)S(1)} %bitcast.241, f32[2560]{0:T(1024)S(1)} %copy-done.58), kind=kOutput, calls=%fused_computation.4 | convolution fusion | flops 12090212352 | bytes 24389636 | tf_op jit(solution)/shard_map/rd,rf->df/dot_general | solution.py:642
  431.8 4.5 add_convert_fusion.6
  436.3 2.2 add_convert_fusion.4
  438.5 10.8 %all-to-all-done.4 = bf16[8,8,40,768]{3,2,1,0:T(8,128)(2,1)} async-done(((bf16[8,8,40,768]{3,2,1,0:T(8,128)(2,1)}), bf16[8,8,40,768]{3,2,1,0:T(8,128)(2,1)}, u32[]{:S(2)}, u32[]{:S(2)}) %all-to-all-start.4) | async-done | bytes 3932192 | tf_op jit(solution)/shard_map/all_to_all | solution.py:553
  449.3 4.9 all-to-all-start.5
  454.3 3.4 fusion.9
  457.7 4.6 multiply_reduce_fusion
  462.3 2.5 convert_add_fusion
  464.9 2.6 convolution_convert_fusion.4.g_ref
  467.5 38.6 %attend_back.1 = (bf16[1024,768]{1,0:T(8,128)(2,1)}, bf16[1024,768]{1,0:T(8,128)(2,1)}, bf16[1024,768]{1,0:T(8,128)(2,1)}) custom-call(s32[1]{0:T(128)} %bitcast.1.start_ref, bf16[1024,2304]{1,0:T(8,128)(2,1)} %convolution_convert_fusion.1.q_ref.k_ref.v_ref, bf16[1024,2304]{1,0:T(8,128)(2,1)} %convolution_convert_fusion.1.q_ref.k_ref.v_ref, ...), custom_call_target="tpu_custom_call" | custom-call | flops 4026531840 | bytes 15728640 | tf_op jit(solution)/shard_map/attend_back/pallas_call | solution.py:190
  509.4 8.2 %fusion.24 = (f32[1024]{0:T(1024)}, bf16[768]{0:T(1024)(128)(2,1)S(1)}, f32[1024]{0:T(1024)}, bf16[768]{0:T(1024)(128)(2,1)S(1)}, f32[1024,768]{1,0:T(8,128)}) fusion(bf16[8,128,768]{2,1,0:T(8,128)(2,1)} %all-to-all-done, f32[768]{0:T(1024)S(1)} %copy-done.31, f32[1024]{0:T(1024)S(1)} %copy-done.35, f32[1024]{0:T(1024)S(1)} %copy-done.33, ...), kind=kOutput, calls=%fused_computation.42 | convolution fusion | flops 3631739392 | bytes 12998656 | tf_op jit(solution)/shard_map/re,de->rd/dot_general | solution.py:693
  519.8 4.0 convolution_convert_fusion.5
  524.0 4.1 convolution_convert_fusion.2
  528.5 2.4 constant_dynamic-slice_fusion.3
  535.5 3.0 add_convert_fusion.3
  539.9 3.9 fusion.28
  543.8 17.6 %collective-permute-done.14.refs_1_ = bf16[768,768]{1,0:T(8,128)(2,1)} collective-permute-done((bf16[768,768]{1,0:T(8,128)(2,1)}, bf16[768,768]{1,0:T(8,128)(2,1)}, u32[]{:S(2)}, u32[]{:S(2)}) %collective-permute-start.14) | collective-permute-done | bytes 1179680 | tf_op jit(solution)/shard_map/ppermute | solution.py:516
  561.4 25.3 %collective-permute-done.15.refs_3_ = bf16[768,768]{1,0:T(8,128)(2,1)} collective-permute-done((bf16[768,768]{1,0:T(8,128)(2,1)}, bf16[768,768]{1,0:T(8,128)(2,1)}, u32[]{:S(2)}, u32[]{:S(2)}) %collective-permute-start.15) | collective-permute-done | bytes 1179680 | tf_op jit(solution)/shard_map/ppermute | solution.py:516
  586.7 6.0 all-to-all-start.6
  593.3 3.5 copy.189
  596.8 2.6 copy.188
  599.4 13.1 %collective-permute-done.13 = bf16[192,3200]{1,0:T(8,128)(2,1)} collective-permute-done((bf16[192,3200]{1,0:T(8,128)(2,1)}, bf16[192,3200]{1,0:T(8,128)(2,1)}, u32[]{:S(2)}, u32[]{:S(2)}) %collective-permute-start.13) | collective-permute-done | bytes 1228832 | tf_op jit(solution)/shard_map/ppermute | solution.py:516
  612.5 2.6 copy.190
  615.1 4.6 add_convert_fusion
  619.7 2.6 copy.191.block_ref
  623.6 6.0 deal.1
  629.6 3.4 fusion.7
  634.6 6.2 all-to-all-start.7
  640.8 2.7 copy.192
  643.4 2.4 copy.193.basis_ref
  645.8 21.5 %refresh.1 = (f32[1,2,768,768]{3,2,1,0:T(8,128)}, f32[1,2,768,768]{3,2,1,0:T(8,128)}, f32[1,2,768,768]{3,2,1,0:T(8,128)}, f32[1,2,768,768]{3,2,1,0:T(8,128)}, f32[1,2,768,768]{3,2,1,0:T(8,128)}) custom-call(s32[1]{0:T(128)} %bitcast.60.flag_ref, bf16[768,768]{1,0:T(8,128)(2,1)} %copy.193.basis_ref, bf16[768,768]{1,0:T(8,128)(2,1)} %bitcast.235, ...), custom_call_target="tpu_custom_call" | custom-call | flops 3623878656 | bytes 44826624 | tf_op jit(solution)/shard_map/refresh/pallas_call | solution.py:304
  667.3 4.0 all-to-all-done.7
  674.9 4.2 collective-permute-done.17
  679.1 4.4 all-to-all-start.8
  690.2 4.6 fusion.30
  694.8 3.7 fusion.67
  698.5 6.2 fusion.29
  704.7 16.7 %all-to-all-done.8 = bf16[8,128,768]{2,1,0:T(8,128)(2,1)} async-done(((bf16[8,128,768]{2,1,0:T(8,128)(2,1)}), bf16[8,128,768]{2,1,0:T(8,128)(2,1)}, u32[]{:S(2)}, u32[]{:S(2)}) %all-to-all-start.8) | async-done | bytes 1572896 | tf_op jit(solution)/shard_map/all_to_all | solution.py:489
  721.3 2.7 copy.226
  724.0 2.7 copy.227
  (258 shorter events, 90.6 us)
Async XLA Ops:
  0.7 134.4 %copy-start = (bf16[768,2304]{1,0:T(8,128)(2,1)S(1)}, bf16[768,2304]{1,0:T(8,128)(2,1)}, u32[]{:S(2)}) copy-start(bf16[768,2304]{1,0:T(8,128)(2,1)} %param.28) | copy-start | bytes 10616836
  0.7 7.6 %copy-start.45 = (s32[8,128,2]{1,2,0:T(2,128)S(1)}, s32[8,128,2]{1,2,0:T(2,128)}, u32[]{:S(2)}) copy-start(s32[8,128,2]{1,2,0:T(2,128)} %param.34) | copy-start | bytes 24580
  0.7 44.8 %all-to-all-start = ((bf16[8,128,768]{2,1,0:T(8,128)(2,1)}), bf16[8,128,768]{2,1,0:T(8,128)(2,1)}, u32[]{:S(2)}, u32[]{:S(2)}) async-start(bf16[8,128,768]{2,1,0:T(8,128)(2,1)} %param.26), calls=%async_computation | async-start | bytes 3145728 | tf_op jit(solution)/shard_map/all_to_all | solution.py:489
  13.4 10.2 %copy-start.23 = (s32[8,128,2]{1,2,0:T(2,128)}, s32[8,128,2]{1,2,0:T(2,128)S(1)}, u32[]{:S(2)}) copy-start(s32[8,128,2]{1,2,0:T(2,128)S(1)} %compare_select_fusion.1) | copy-start | bytes 24580
  14.0 20.7 %collective-permute-start = (s32[2,128]{1,0:T(2,128)}, s32[2,128]{1,0:T(2,128)S(1)}, u32[]{:S(2)}, u32[]{:S(2)}) collective-permute-start(s32[2,128]{1,0:T(2,128)} %get-tuple-element.138), channel_id=1, source_target_pairs={{0,7},{1,0},{2,1},{3,2},{4,3},{5,4},{6,5},{7,6},{8,15},{9,8},{10,9... | collective-permute-start | bytes 3080 | tf_op jit(solution)/shard_map/ppermute | solution.py:502
  18.8 31.3 %collective-permute-start.1 = (s32[2,128]{1,0:T(2,128)}, s32[2,128]{1,0:T(2,128)}, u32[]{:S(2)}, u32[]{:S(2)}) collective-permute-start(s32[2,128]{1,0:T(2,128)} %get-tuple-element.137), channel_id=1, source_target_pairs={{0,6},{1,7},{2,0},{3,1},{4,2},{5,3},{6,4},{7,5},{8,14},{9,15},{10,... | collective-permute-start | bytes 3080 | tf_op jit(solution)/shard_map/ppermute | solution.py:502
  19.3 34.5 %collective-permute-start.2 = (s32[2,128]{1,0:T(2,128)}, s32[2,128]{1,0:T(2,128)}, u32[]{:S(2)}, u32[]{:S(2)}) collective-permute-start(s32[2,128]{1,0:T(2,128)} %get-tuple-element.136), channel_id=1, source_target_pairs={{0,5},{1,6},{2,7},{3,0},{4,1},{5,2},{6,3},{7,4},{8,13},{9,14},{10,... | collective-permute-start | bytes 3080 | tf_op jit(solution)/shard_map/ppermute | solution.py:502
  19.3 35.7 %collective-permute-start.3 = (s32[2,128]{1,0:T(2,128)}, s32[2,128]{1,0:T(2,128)}, u32[]{:S(2)}, u32[]{:S(2)}) collective-permute-start(s32[2,128]{1,0:T(2,128)} %get-tuple-element.135), channel_id=1, source_target_pairs={{0,4},{1,5},{2,6},{3,7},{4,0},{5,1},{6,2},{7,3},{8,12},{9,13},{10,... | collective-permute-start | bytes 3080 | tf_op jit(solution)/shard_map/ppermute | solution.py:502
  22.3 34.1 %collective-permute-start.4 = (s32[2,128]{1,0:T(2,128)}, s32[2,128]{1,0:T(2,128)}, u32[]{:S(2)}, u32[]{:S(2)}) collective-permute-start(s32[2,128]{1,0:T(2,128)} %get-tuple-element.134), channel_id=1, source_target_pairs={{0,3},{1,4},{2,5},{3,6},{4,7},{5,0},{6,1},{7,2},{8,11},{9,12},{10,... | collective-permute-start | bytes 3080 | tf_op jit(solution)/shard_map/ppermute | solution.py:502
  34.7 22.8 %collective-permute-start.5 = (s32[2,128]{1,0:T(2,128)}, s32[2,128]{1,0:T(2,128)S(1)}, u32[]{:S(2)}, u32[]{:S(2)}) collective-permute-start(s32[2,128]{1,0:T(2,128)} %get-tuple-element.133), channel_id=1, source_target_pairs={{0,2},{1,3},{2,4},{3,5},{4,6},{5,7},{6,0},{7,1},{8,10},{9,11},{10,... | collective-permute-start | bytes 3080 | tf_op jit(solution)/shard_map/ppermute | solution.py:502
  45.5 130.2 %all-to-all-start.1 = ((bf16[8,8,40,768]{3,2,1,0:T(8,128)(2,1)}), bf16[8,8,40,768]{3,2,1,0:T(8,128)(2,1)}, u32[]{:S(2)}, u32[]{:S(2)}) async-start(bf16[8,8,40,768]{3,2,1,0:T(8,128)(2,1)} %send_rows.3), calls=%async_computation.1 | async-start | bytes 7864320 | tf_op jit(solution)/shard_map/all_to_all | solution.py:553
  50.0 83.0 %copy-start.30 = (f32[768]{0:T(1024)S(1)}, f32[768]{0:T(1024)}, u32[]{:S(2)}) copy-start(f32[768]{0:T(1024)} %get-tuple-element.147) | copy-start | bytes 9220
  50.0 83.0 %copy-start.51 = (f32[768]{0:T(1024)S(1)}, f32[768]{0:T(1024)}, u32[]{:S(2)}) copy-start(f32[768]{0:T(1024)} %get-tuple-element.90) | copy-start | bytes 9220
  50.1 67.7 %collective-permute-start.6 = (s32[2,128]{1,0:T(2,128)}, s32[2,128]{1,0:T(2,128)S(1)}, u32[]{:S(2)}, u32[]{:S(2)}) collective-permute-start(s32[2,128]{1,0:T(2,128)} %get-tuple-element.132), channel_id=1, source_target_pairs={{0,1},{1,2},{2,3},{3,4},{4,5},{5,6},{6,7},{7,0},{8,9},{9,10},{10,1... | collective-permute-start | bytes 3080 | tf_op jit(solution)/shard_map/ppermute | solution.py:502
  128.7 72.7 %copy-start.24 = (s32[8,2,128]{2,1,0:T(2,128)}, s32[8,2,128]{2,1,0:T(2,128)S(1)}, u32[]{:S(2)}) copy-start(s32[8,2,128]{2,1,0:T(2,128)S(1)} %get-tuple-element.99) | copy-start | bytes 24580
  135.1 5.5 copy-start.12
  175.7 110.8 %all-to-all-start.2 = ((bf16[8,8,40,768]{3,2,1,0:T(8,128)(2,1)}), bf16[8,8,40,768]{3,2,1,0:T(8,128)(2,1)}, u32[]{:S(2)}, u32[]{:S(2)}) async-start(bf16[8,8,40,768]{3,2,1,0:T(8,128)(2,1)} %send_rows.2), calls=%async_computation.2 | async-start | bytes 7864320 | tf_op jit(solution)/shard_map/all_to_all | solution.py:553
  198.6 3.9 copy-start.36
  198.6 4.4 copy-start.40
  286.5 71.4 %all-to-all-start.3 = ((bf16[8,128,768]{2,1,0:T(8,128)(2,1)}), bf16[8,128,768]{2,1,0:T(8,128)(2,1)}, u32[]{:S(2)}, u32[]{:S(2)}) async-start(bf16[8,128,768]{2,1,0:T(8,128)(2,1)} %param.27), calls=%async_computation.3 | async-start | bytes 3145728 | tf_op jit(solution)/shard_map/all_to_all | solution.py:489
  357.8 91.5 %all-to-all-start.4 = ((bf16[8,8,40,768]{3,2,1,0:T(8,128)(2,1)}), bf16[8,8,40,768]{3,2,1,0:T(8,128)(2,1)}, u32[]{:S(2)}, u32[]{:S(2)}) async-start(bf16[8,8,40,768]{3,2,1,0:T(8,128)(2,1)} %bitcast.242), calls=%async_computation.4 | async-start | bytes 7864320 | tf_op jit(solution)/shard_map/all_to_all | solution.py:553
  386.6 45.2 %collective-permute-start.8 = (bf16[768,768]{1,0:T(8,128)(2,1)}, bf16[768,768]{1,0:T(8,128)(2,1)}, u32[]{:S(2)}, u32[]{:S(2)}) collective-permute-start(bf16[768,768]{1,0:T(8,128)(2,1)} %get-tuple-element.110), channel_id=1, source_target_pairs={{0,8},{8,0},{16,24},{24,16},{1,9},{9,1},{17,25},{25,17},{2,10},{10... | collective-permute-start | bytes 3538952 | tf_op jit(solution)/shard_map/ppermute | solution.py:519
  386.6 18.6 %copy-start.11 = (bf16[1,8,8,40,768]{4,3,2,1,0:T(8,128)(2,1)S(1)}, bf16[1,8,8,40,768]{4,3,2,1,0:T(8,128)(2,1)}, u32[]{:S(2)}) copy-start(bf16[1,8,8,40,768]{4,3,2,1,0:T(8,128)(2,1)} %copy-done.10) | copy-start | bytes 11796484
  386.6 18.6 %copy-start.58 = (f32[2560]{0:T(1024)S(1)}, f32[2560]{0:T(1024)}, u32[]{:S(2)}) copy-start(f32[2560]{0:T(1024)} %mul.325) | copy-start | bytes 30724
  386.6 45.2 %collective-permute-start.7 = (bf16[768,768]{1,0:T(8,128)(2,1)}, bf16[768,768]{1,0:T(8,128)(2,1)}, u32[]{:S(2)}, u32[]{:S(2)}) collective-permute-start(bf16[768,768]{1,0:T(8,128)(2,1)} %get-tuple-element.111), channel_id=1, source_target_pairs={{0,8},{8,0},{16,24},{24,16},{1,9},{9,1},{17,25},{25,17},{2,10},{10... | collective-permute-start | bytes 3538952 | tf_op jit(solution)/shard_map/ppermute | solution.py:519
  429.3 6.9 collective-permute-start.10
  429.4 6.9 collective-permute-start.9
  431.8 4.5 copy-start.9
  449.3 4.9 copy-start.38
  449.3 137.4 %all-to-all-start.5 = ((bf16[8,8,40,768]{3,2,1,0:T(8,128)(2,1)}), bf16[8,8,40,768]{3,2,1,0:T(8,128)(2,1)}, u32[]{:S(2)}, u32[]{:S(2)}) async-start(bf16[8,8,40,768]{3,2,1,0:T(8,128)(2,1)} %bitcast.239), calls=%async_computation.5 | async-start | bytes 7864320 | tf_op jit(solution)/shard_map/all_to_all | solution.py:553
  454.2 3.4 copy-start.2
  454.2 3.4 copy-start.20
  509.3 8.2 %copy-start.17 = (bf16[1024,2304]{1,0:T(8,128)(2,1)}, bf16[1024,2304]{1,0:T(8,128)(2,1)S(1)}, u32[]{:S(2)}) copy-start(bf16[1024,2304]{1,0:T(8,128)(2,1)S(1)} %constant_dynamic-update-slice_fusion.16) | copy-start | bytes 14155780
  509.3 8.2 %copy-start.59 = (bf16[768]{0:T(1024)(128)(2,1)S(1)}, bf16[768]{0:T(1024)(128)(2,1)}, u32[]{:S(2)}) copy-start(bf16[768]{0:T(1024)(128)(2,1)} %get-tuple-element.77) | copy-start | bytes 4612
  509.3 8.3 %copy-start.28 = (bf16[768,8]{0,1:T(8,128)(2,1)S(1)}, bf16[768,8]{0,1:T(8,128)(2,1)}, u32[]{:S(2)}) copy-start(bf16[768,8]{0,1:T(8,128)(2,1)} %convolution_convert_fusion.8) | copy-start | bytes 36868
  519.8 4.0 copy-start.13
  519.8 4.2 copy-start.18
  524.0 4.1 copy-start.16
  528.5 3.7 copy-start.5
  532.2 7.7 %copy-start.60 = (f32[1024]{0:T(1024)S(1)}, f32[1024]{0:T(1024)}, u32[]{:S(2)}) copy-start(f32[1024]{0:T(1024)} %get-tuple-element.82) | copy-start | bytes 12292
  532.2 3.3 collective-permute-start.12
  532.2 7.7 %copy-start.7 = (f32[1024,768]{1,0:T(8,128)S(1)}, f32[1024,768]{1,0:T(8,128)}, u32[]{:S(2)}) copy-start(f32[1024,768]{1,0:T(8,128)} %copy-done.6) | copy-start | bytes 9437188
  532.2 29.2 %collective-permute-start.14 = (bf16[768,768]{1,0:T(8,128)(2,1)}, bf16[768,768]{1,0:T(8,128)(2,1)}, u32[]{:S(2)}, u32[]{:S(2)}) collective-permute-start(bf16[768,768]{1,0:T(8,128)(2,1)} %get-tuple-element.106), channel_id=1, source_target_pairs={{0,16},{8,24},{16,0},{24,8},{1,17},{9,25},{17,1},{25,9},{2,18},{10... | collective-permute-start | bytes 3538952 | tf_op jit(solution)/shard_map/ppermute | solution.py:516
  533.6 53.0 %collective-permute-start.15 = (bf16[768,768]{1,0:T(8,128)(2,1)}, bf16[768,768]{1,0:T(8,128)(2,1)}, u32[]{:S(2)}, u32[]{:S(2)}) collective-permute-start(bf16[768,768]{1,0:T(8,128)(2,1)} %get-tuple-element.104), channel_id=1, source_target_pairs={{0,16},{8,24},{16,0},{24,8},{1,17},{9,25},{17,1},{25,9},{2,18},{10... | collective-permute-start | bytes 3538952 | tf_op jit(solution)/shard_map/ppermute | solution.py:516
  534.3 62.5 %collective-permute-start.11 = (bf16[192,3200]{1,0:T(8,128)(2,1)}, bf16[192,3200]{1,0:T(8,128)(2,1)}, u32[]{:S(2)}, u32[]{:S(2)}) collective-permute-start(bf16[192,3200]{1,0:T(8,128)(2,1)} %get-tuple-element.101), channel_id=1, source_target_pairs={{0,8},{8,0},{16,24},{24,16},{1,9},{9,1},{17,25},{25,17},{2,10},{10... | collective-permute-start | bytes 3686408 | tf_op jit(solution)/shard_map/ppermute | solution.py:519
  538.5 74.1 %collective-permute-start.13 = (bf16[192,3200]{1,0:T(8,128)(2,1)}, bf16[192,3200]{1,0:T(8,128)(2,1)}, u32[]{:S(2)}, u32[]{:S(2)}) collective-permute-start(bf16[192,3200]{1,0:T(8,128)(2,1)} %add_convert_fusion.3), channel_id=1, source_target_pairs={{0,16},{8,24},{16,0},{24,8},{1,17},{9,25},{17,1},{25,9},{2,18},{10... | collective-permute-start | bytes 3686408 | tf_op jit(solution)/shard_map/ppermute | solution.py:516
  543.8 48.9 %copy-start.62 = (s32[8]{0:T(128)S(1)}, s32[8]{0:T(128)}, u32[]{:S(2)}) copy-start(s32[8]{0:T(128)} %param.37) | copy-start | bytes 100
  586.7 47.9 %all-to-all-start.6 = ((bf16[8,128,768]{2,1,0:T(8,128)(2,1)}), bf16[8,128,768]{2,1,0:T(8,128)(2,1)}, u32[]{:S(2)}, u32[]{:S(2)}) async-start(bf16[8,128,768]{2,1,0:T(8,128)(2,1)} %bitcast.238), calls=%async_computation.6 | async-start | bytes 3145728 | tf_op jit(solution)/shard_map/all_to_all | solution.py:489
  619.7 9.9 %copy-start.39 = (s32[8,1,128]{2,1,0:T(1,128)S(1)}, s32[8,1,128]{2,1,0:T(1,128)}, u32[]{:S(2)}) copy-start(s32[8,1,128]{2,1,0:T(1,128)} %copy-done.36) | copy-start | bytes 12292
  619.7 9.9 %copy-start.42 = (s32[8,1,128]{2,1,0:T(1,128)S(1)}, s32[8,1,128]{2,1,0:T(1,128)}, u32[]{:S(2)}) copy-start(s32[8,1,128]{2,1,0:T(1,128)} %copy-done.40) | copy-start | bytes 12292
  619.7 9.9 %copy-start.53 = (f32[8,1,128]{2,1,0:T(1,128)S(1)}, f32[8,1,128]{2,1,0:T(1,128)}, u32[]{:S(2)}) copy-start(f32[8,1,128]{2,1,0:T(1,128)} %copy-done.52) | copy-start | bytes 12292
  619.7 9.9 %copy-start.55 = (f32[8,1,128]{2,1,0:T(1,128)S(1)}, f32[8,1,128]{2,1,0:T(1,128)}, u32[]{:S(2)}) copy-start(f32[8,1,128]{2,1,0:T(1,128)} %copy-done.54) | copy-start | bytes 12292
  634.6 36.7 %all-to-all-start.7 = ((bf16[8,208,384]{2,1,0:T(8,128)(2,1)}), bf16[8,208,384]{2,1,0:T(8,128)(2,1)}, u32[]{:S(2)}, u32[]{:S(2)}) async-start(bf16[8,208,384]{2,1,0:T(8,128)(2,1)} %deal.1), calls=%async_computation.7 | async-start | bytes 2555904 | tf_op jit(solution)/shard_map/all_to_all | solution.py:553
  673.5 5.6 collective-permute-start.17
  674.9 8.7 %collective-permute-start.16 = (bf16[208,384]{1,0:T(8,128)(2,1)}, bf16[208,384]{1,0:T(8,128)(2,1)}, u32[]{:S(2)}, u32[]{:S(2)}) collective-permute-start(bf16[208,384]{1,0:T(8,128)(2,1)} %reduce_sum.242), channel_id=1, source_target_pairs={{0,8},{8,0},{16,24},{24,16},{1,9},{9,1},{17,25},{25,17},{2,10},{10... | collective-permute-start | bytes 479240 | tf_op jit(solution)/shard_map/ppermute | solution.py:519
  679.1 4.5 collective-permute-start.18
  679.1 42.3 %all-to-all-start.8 = ((bf16[8,128,768]{2,1,0:T(8,128)(2,1)}), bf16[8,128,768]{2,1,0:T(8,128)(2,1)}, u32[]{:S(2)}, u32[]{:S(2)}) async-start(bf16[8,128,768]{2,1,0:T(8,128)(2,1)} %bitcast.237), calls=%async_computation.8 | async-start | bytes 3145728 | tf_op jit(solution)/shard_map/all_to_all | solution.py:489
  683.5 5.3 copy-start.48
  683.5 5.2 copy-start.49
  683.5 5.2 copy-start.56
  683.5 5.2 copy-start.57
  683.5 5.9 copy-start.22
  683.5 5.9 copy-start.46
  683.5 5.9 copy-start.47
  (27 other events, 56.0 us)

commit v2 on v1

--- a/solution.py
+++ b/solution.py
@@ -238,7 +238,7 @@
         gate_grad = here if gate_grad is None else gate_grad + here
         inputs = add if inputs is None else inputs + add
     input_ref[...] = inputs.astype(low)
-    gate_grad_ref[0] = gate_grad.T
+    gate_grad_ref[...] = gate_grad.T
 
 
 def expert_stage(x, u, w):
@@ -255,7 +255,7 @@
             jax.ShapeDtypeStruct((rows, hidden), low),
             jax.ShapeDtypeStruct((rows, hidden), low),
             jax.ShapeDtypeStruct((rows, width), low),
-            jax.ShapeDtypeStruct((rows // TILE, 1, TILE), wide),
+            jax.ShapeDtypeStruct((1, rows), wide),
         ),
         in_specs=[
             row_block(width),
@@ -266,7 +266,7 @@
             row_block(hidden),
             row_block(hidden),
             row_block(width),
-            pl.BlockSpec((1, 1, TILE), lambda i: (i, 0, 0)),
+            pl.BlockSpec((1, TILE), lambda i: (0, i)),
         ),
         cost_estimate=pl.CostEstimate(
             flops=4 * rows * width * hidden,
@@ -324,15 +324,25 @@
     )(flag, basis, basis.T, *terms[0], *terms[1], master, first, second, average)
 
 
+def turn_small(small, count):
+    lane = lax.broadcasted_iota(jnp.int32, (count, small.shape[1]), 1)
+    row = lax.broadcasted_iota(jnp.int32, (count, small.shape[1]), 0)
+    return dot_low((lane == row).astype(wide), small, ROW_ROW).astype(low)
+
+
 def deal_kernel(which_ref, block_ref, small_ref, out_ref):
     height = block_ref.shape[0]
+    extra = out_ref.shape[1] - height
     out_ref[0, :height] = block_ref[...]
-    out_ref[0, height:] = small_ref[...]
-
-
-def deal(which, rows, small, count):
-    height, extra, block_width = rows.shape[0], small.shape[0], small.shape[1]
+    out_ref[0, height:] = jnp.zeros((extra, out_ref.shape[2]), low)
+    out_ref[0, height:, :height] = turn_small(small_ref[...], extra)
+
+
+def deal(which, rows, extra, block_width, count):
+    height, total = rows.shape
     if block_width % 128:
+        small = turn_small(rows[:, block_width * count :], extra)
+        small = jnp.pad(small, ((0, 0), (0, block_width - height)))
         return jnp.stack(
             [
                 jnp.concatenate(
@@ -344,6 +354,7 @@
                 for s in range(count)
             ]
         )
+    lanes = total - block_width * count
     return pl.pallas_call(
         deal_kernel,
         grid_spec=pltpu.PrefetchScalarGridSpec(
@@ -351,13 +362,13 @@
             grid=(count,),
             in_specs=[
                 pl.BlockSpec((height, block_width), lambda s, which: (0, which[s])),
-                pl.BlockSpec((extra, block_width), lambda s, which: (0, 0)),
+                pl.BlockSpec((height, lanes), lambda s, which: (0, total // lanes - 1)),
             ],
             out_specs=pl.BlockSpec((1, height + extra, block_width), lambda s, which: (s, 0, 0)),
         ),
         out_shape=jax.ShapeDtypeStruct((count, height + extra, block_width), rows.dtype),
         name="deal",
-    )(which, rows, small)
+    )(which, rows, rows)
 
 
 def trade_kernel(count, in_ref, out_ref, landed, send_sem, recv_sem):
@@ -719,15 +730,12 @@
         [grad_w_project.astype(low), grad_w_output.astype(low), small], axis=1
     )
     half_rows = halve(grad_full, 0, cut_dp(grad_full, 0, 1 - core))
-    my_rows = sum(term.astype(wide) for term in spread(half_rows)).astype(low)
+    dp_terms, output_seq = lax.optimization_barrier((spread(half_rows), output_seq))
+    my_rows = sum(term.astype(wide) for term in dp_terms).astype(low)
     height = my_rows.shape[0]
     small_rows = -(-small_width // 16) * 16
-    small = jnp.pad(
-        my_rows[:, block_width * expert_count :][:, :small_width].T,
-        ((0, small_rows - small_width), (0, block_width - height)),
-    )
-    my_rows = deal(which_block, my_rows, small, expert_count)
-    my_rows = after(exchange(after(my_rows, input_grad, output_seq)), expert_grad)
+    my_rows = deal(which_block, my_rows, small_rows, block_width, expert_count)
+    my_rows = after(exchange(after(my_rows, input_grad)), expert_grad)
     my_rows_done = my_rows
     pieces = gather_dp(jnp.sum(my_rows.astype(wide), axis=0).astype(low))
     block_grad = jnp.concatenate([piece[:height] for piece in pieces]).astype(wide)

time: 738 us -> 735 us (level)
  local copies, waits for them, and re-layouts: 79.9 us -> 69.5 us
  waiting for transfers between devices: 223 us -> 231 us
    ppermute x4, waiting for transfers between devices: 60.2 us -> 70.8 us  [dp_move(): lax.ppermute(value, 'dp', [(d, (d + 2 * shift) % dp_count) for d in range...]
  transfers between devices with their start and end apart: 28 -> 28, of which waited for: 12 -> 11; matrix products, arithmetic and copies ran while one was open for 33% -> 31% of each run, Pallas kernels for 22% -> 22%
where the time goes in v2:
time: 735 us; the launch traced here: 724 us
  waiting for transfers between devices  231 us (31%)
  Pallas kernels  161 us (22%)
  matrix products  127 us (17%)
  starting transfers between devices  82.7 us (11%)
  local copies, waits for them, and re-layouts  69.5 us (9%)
  other arithmetic  50.1 us (7%)
    ppermute x4, waiting for transfers between devices, dp_move(): lax.ppermute(value, 'dp', [(d, (d + 2 * shift) % dp_count) for d in range...  70.8 us
    all_to_all x5, waiting for transfers between devices, exchange(): lax.all_to_all(value, 'expert', split_axis=0, concat_axis=0, tiled=True)  69.7 us
    ppermute x7, waiting for transfers between devices, ring(): rows.append(lax.ppermute(given, 'expert', moves))  63.9 us
    pallas_call x1, Pallas kernels, expert_stage(): pl.pallas_call(expert_kernel, grid=(rows // TILE,), out_shape=(jax.ShapeD...  50.4 us
    all_to_all x5, starting transfers between devices, exchange(): lax.all_to_all(value, 'expert', split_axis=0, concat_axis=0, tiled=True)  42.9 us
    pallas_call x1, Pallas kernels, attend_back(): pl.pallas_call(functools.partial(attend_back_kernel, whole), grid=(pairs,...  38.2 us
    unnamed x149, local copies, waits for them, and re-layouts  33.6 us
    all_to_all x4, waiting for transfers between devices, swap(): lax.all_to_all(value, 'expert', split_axis=0, concat_axis=0, tiled=True,...  27 us
  transfers between devices with their start and end apart: 28, of which 11 were waited for; matrix products, arithmetic and copies ran while one was open for 31% of the time, Pallas kernels for 22%

profile of v2, /device:TPU:0, one launch (start us, length us, event | category | flops | bytes accessed | tf_op | source)
XLA Modules:
  0.0 724.5 jit_solution(8624658006814059890)
XLA Ops:
  0.7 7.6 %all-to-all-start = ((bf16[8,128,768]{2,1,0:T(8,128)(2,1)}), bf16[8,128,768]{2,1,0:T(8,128)(2,1)}, u32[]{:S(2)}, u32[]{:S(2)}) async-start(bf16[8,128,768]{2,1,0:T(8,128)(2,1)} %param.26), calls=%async_computation | async-start | bytes 3145728 | tf_op jit(solution)/shard_map/all_to_all | solution.py:500
  14.0 4.7 collective-permute-start
  19.3 2.9 collective-permute-start.3
  23.7 6.9 send_rows.3
  30.5 4.2 collective-permute-done
  35.3 10.2 %all-to-all-done = bf16[8,128,768]{2,1,0:T(8,128)(2,1)} async-done(((bf16[8,128,768]{2,1,0:T(8,128)(2,1)}), bf16[8,128,768]{2,1,0:T(8,128)(2,1)}, u32[]{:S(2)}, u32[]{:S(2)}) %all-to-all-start) | async-done | bytes 1572896 | tf_op jit(solution)/shard_map/all_to_all | solution.py:500
  45.5 4.5 all-to-all-start.1
  50.1 2.5 collective-permute-start.6
  58.1 59.7 %collective-permute-done.6 = s32[2,128]{1,0:T(2,128)S(1)} collective-permute-done((s32[2,128]{1,0:T(2,128)}, s32[2,128]{1,0:T(2,128)S(1)}, u32[]{:S(2)}, u32[]{:S(2)}) %collective-permute-start.6) | collective-permute-done | bytes 1056 | tf_op jit(solution)/shard_map/ppermute | solution.py:513
  130.4 2.0 fusion.15
  133.0 2.0 fusion.22
  135.1 5.5 convolution_convert_fusion.1.q_ref.k_ref.v_ref
  140.5 22.0 %attend.1 = (bf16[1024,768]{1,0:T(8,128)(2,1)}, f32[1024,768]{1,0:T(8,128)}) custom-call(s32[1]{0:T(128)} %bitcast.3.start_ref, bf16[1024,2304]{1,0:T(8,128)(2,1)} %convolution_convert_fusion.1.q_ref.k_ref.v_ref, bf16[1024,2304]{1,0:T(8,128)(2,1)} %convolution_convert_fusion.1.q_ref.k_ref.v_ref, bf16[1024,2304]{1,0:T(8,128)(2,1)} %convolution_convert_fusion.1.q_ref.k_ref.v_ref), custom_call_target="tpu_custom_call" | custom-call | flops 1610612736 | bytes 9437184 | tf_op jit(solution)/shard_map/attend/pallas_call | solution.py:165
  162.6 3.8 fusion.115
  168.8 6.9 send_rows.2
  175.6 22.2 %all-to-all-start.2 = ((bf16[8,8,40,768]{3,2,1,0:T(8,128)(2,1)}), bf16[8,8,40,768]{3,2,1,0:T(8,128)(2,1)}, u32[]{:S(2)}, u32[]{:S(2)}) async-start(bf16[8,8,40,768]{3,2,1,0:T(8,128)(2,1)} %send_rows.2), calls=%async_computation.2 | async-start | bytes 7864320 | tf_op jit(solution)/shard_map/all_to_all | solution.py:564
  198.6 2.7 convolution_bitcast_fusion.1
  207.8 2.4 copy.120
  210.2 1.9 copy-done.9
  212.1 17.5 %convolution_convert_fusion.u_ref = bf16[2560,3072]{1,0:T(8,128)(2,1)} fusion(bf16[2560,768]{1,0:T(8,128)(2,1)S(1)} %bitcast.238, bf16[1,2,768,3072]{3,2,1,0:T(8,128)(2,1)} %w_ref.1), kind=kOutput, calls=%fused_computation.1 | convolution fusion | flops 12087459840 | bytes 24379392 | tf_op jit(solution)/shard_map/dot_general | solution.py:612
  229.7 56.7 %all-to-all-done.2 = bf16[8,8,40,768]{3,2,1,0:T(8,128)(2,1)} async-done(((bf16[8,8,40,768]{3,2,1,0:T(8,128)(2,1)}), bf16[8,8,40,768]{3,2,1,0:T(8,128)(2,1)}, u32[]{:S(2)}, u32[]{:S(2)}) %all-to-all-start.2) | async-done | bytes 3932192 | tf_op jit(solution)/shard_map/all_to_all | solution.py:564
  286.4 4.3 all-to-all-start.3
  293.4 50.4 %expert_stage.1 = (bf16[2560,3072]{1,0:T(8,128)(2,1)}, bf16[2560,3072]{1,0:T(8,128)(2,1)}, bf16[2560,768]{1,0:T(8,128)(2,1)}, f32[1,2560]{1,0:T(1,128)}) custom-call(bf16[2560,768]{1,0:T(8,128)(2,1)} %bitcast.32.x_ref, bf16[2560,3072]{1,0:T(8,128)(2,1)} %convolution_convert_fusion.u_ref, bf16[1,2,768,3072]{3,2,1,0:T(8,128)(2,1)} %w_ref.1), custom_call_target="tpu_custom_call" | custom-call | flops 24159191040 | bytes 47185920 | tf_op jit(solution)/shard_map/expert_stage/pallas_call | solution.py:251
  347.9 8.3 %trade.1 = f32[8,8,128]{2,1,0:T(8,128)} custom-call(f32[8,8,128]{2,1,0:T(8,128)} %bitcast.244), custom_call_target="tpu_custom_call" | custom-call | tf_op jit(solution)/shard_map/trade/pallas_call | solution.py:407
  357.5 5.8 all-to-all-start.4
  366.2 17.0 %multiply_convert_fusion.1 = bf16[768,3072]{1,0:T(8,128)(2,1)S(1)} fusion(bf16[2560,3072]{1,0:T(8,128)(2,1)} %get-tuple-element.61, f32[]{:T(128)S(6)} %convert_element_type.224, bf16[2560,768]{1,0:T(8,128)(2,1)} %bitcast.32.x_ref, f32[2560]{0:T(1024)} %mul.334), kind=kOutput, calls=%fused_computation.5 | convolution fusion | flops 12090212352 | bytes 24389636 | tf_op jit(solution)/shard_map/rd,rf->df/dot_general | solution.py:652
  383.2 1.9 constant_dynamic-slice_fusion.6
  386.6 18.1 %convolution_convert_fusion.3 = bf16[2560,768]{1,0:T(8,128)(2,1)} fusion(bf16[2560,3072]{1,0:T(8,128)(2,1)} %get-tuple-element.62, bf16[1,2,768,3072]{3,2,1,0:T(8,128)(2,1)} %w_ref.1), kind=kOutput, calls=%fused_computation.10 | convolution fusion | flops 12081561600 | bytes 24379392 | tf_op jit(solution)/shard_map/rf,df->rd/dot_general | solution.py:647
  404.7 18.4 %multiply_convert_fusion = bf16[768,3072]{1,0:T(8,128)(2,1)} fusion(bf16[2560,3072]{1,0:T(8,128)(2,1)} %get-tuple-element.62, f32[]{:T(128)S(6)} %convert_element_type.224, bf16[2560,768]{1,0:T(8,128)(2,1)S(1)} %bitcast.239, f32[2560]{0:T(1024)S(1)} %copy-done.58), kind=kOutput, calls=%fused_computation.4 | convolution fusion | flops 12090212352 | bytes 24389636 | tf_op jit(solution)/shard_map/rd,rf->df/dot_general | solution.py:653
  427.3 1.9 constant_dynamic-slice_fusion.4
  431.7 4.5 add_convert_fusion.6
  436.2 2.2 add_convert_fusion.4
  438.4 10.4 %all-to-all-done.4 = bf16[8,8,40,768]{3,2,1,0:T(8,128)(2,1)} async-done(((bf16[8,8,40,768]{3,2,1,0:T(8,128)(2,1)}), bf16[8,8,40,768]{3,2,1,0:T(8,128)(2,1)}, u32[]{:S(2)}, u32[]{:S(2)}) %all-to-all-start.4) | async-done | bytes 3932192 | tf_op jit(solution)/shard_map/all_to_all | solution.py:564
  448.9 3.4 fusion.9
  452.3 6.1 multiply_reduce_fusion
  459.0 4.8 all-to-all-start.5
  464.5 3.9 convert_add_fusion
  468.5 2.6 convolution_convert_fusion.4.g_ref
  471.1 38.2 %attend_back.1 = (bf16[1024,768]{1,0:T(8,128)(2,1)}, bf16[1024,768]{1,0:T(8,128)(2,1)}, bf16[1024,768]{1,0:T(8,128)(2,1)}) custom-call(s32[1]{0:T(128)} %bitcast.3.start_ref, bf16[1024,2304]{1,0:T(8,128)(2,1)} %convolution_convert_fusion.1.q_ref.k_ref.v_ref, bf16[1024,2304]{1,0:T(8,128)(2,1)} %convolution_convert_fusion.1.q_ref.k_ref.v_ref, ...), custom_call_target="tpu_custom_call" | custom-call | flops 4026531840 | bytes 15728640 | tf_op jit(solution)/shard_map/attend_back/pallas_call | solution.py:190
  512.5 8.2 %fusion.24 = (f32[1024]{0:T(1024)}, bf16[768]{0:T(1024)(128)(2,1)S(1)}, f32[1024]{0:T(1024)S(1)}, bf16[768]{0:T(1024)(128)(2,1)S(1)}, f32[1024,768]{1,0:T(8,128)}) fusion(bf16[8,128,768]{2,1,0:T(8,128)(2,1)} %all-to-all-done, f32[768]{0:T(1024)S(1)} %copy-done.30, f32[1024]{0:T(1024)S(1)} %copy-done.34, f32[1024]{0:T(1024)S(1)} %copy-done.32, ...), kind=kOutput, calls=%fused_computation.40 | convolution fusion | flops 3631739392 | bytes 12998656 | tf_op jit(solution)/shard_map/re,de->rd/dot_general | solution.py:704
  523.0 3.9 convolution_convert_fusion.5
  527.2 4.3 convolution_convert_fusion.2
  538.2 4.8 fusion.28
  543.0 21.7 %collective-permute-done.14.refs_1_ = bf16[768,768]{1,0:T(8,128)(2,1)} collective-permute-done((bf16[768,768]{1,0:T(8,128)(2,1)}, bf16[768,768]{1,0:T(8,128)(2,1)}, u32[]{:S(2)}, u32[]{:S(2)}) %collective-permute-start.14) | collective-permute-done | bytes 1179680 | tf_op jit(solution)/shard_map/ppermute | solution.py:527
  564.6 24.3 %collective-permute-done.15.refs_3_ = bf16[768,768]{1,0:T(8,128)(2,1)} collective-permute-done((bf16[768,768]{1,0:T(8,128)(2,1)}, bf16[768,768]{1,0:T(8,128)(2,1)}, u32[]{:S(2)}, u32[]{:S(2)}) %collective-permute-start.15) | collective-permute-done | bytes 1179680 | tf_op jit(solution)/shard_map/ppermute | solution.py:527
  589.0 6.0 all-to-all-start.6
  595.0 3.0 add_convert_fusion.2
  600.1 3.4 fusion.7
  605.1 20.7 %collective-permute-done.13 = bf16[192,3200]{1,0:T(8,128)(2,1)S(1)} collective-permute-done((bf16[192,3200]{1,0:T(8,128)(2,1)S(1)}, bf16[192,3200]{1,0:T(8,128)(2,1)S(1)}, u32[]{:S(2)}, u32[]{:S(2)}) %collective-permute-start.13) | collective-permute-done | bytes 1228832 | tf_op jit(solution)/shard_map/ppermute | solution.py:527
  627.1 6.5 deal.1
  633.7 5.7 all-to-all-start.7
  639.4 2.7 copy.127
  642.1 2.4 copy.128.basis_ref
  644.4 21.4 %refresh.1 = (f32[1,2,768,768]{3,2,1,0:T(8,128)}, f32[1,2,768,768]{3,2,1,0:T(8,128)}, f32[1,2,768,768]{3,2,1,0:T(8,128)}, f32[1,2,768,768]{3,2,1,0:T(8,128)}, f32[1,2,768,768]{3,2,1,0:T(8,128)}) custom-call(s32[1]{0:T(128)} %bitcast.59.flag_ref, bf16[768,768]{1,0:T(8,128)(2,1)} %copy.128.basis_ref, bf16[768,768]{1,0:T(8,128)(2,1)} %bitcast.233, ...), custom_call_target="tpu_custom_call" | custom-call | flops 3623878656 | bytes 44826624 | tf_op jit(solution)/shard_map/refresh/pallas_call | solution.py:304
  665.9 2.5 all-to-all-done.7
  668.4 2.2 reduce_sum.242
  672.0 4.1 collective-permute-done.17
  676.2 4.6 all-to-all-start.8
  687.5 4.6 fusion.30
  692.1 3.7 fusion.67
  695.8 6.2 fusion.29
  702.0 16.7 %all-to-all-done.8 = bf16[8,128,768]{2,1,0:T(8,128)(2,1)} async-done(((bf16[8,128,768]{2,1,0:T(8,128)(2,1)}), bf16[8,128,768]{2,1,0:T(8,128)(2,1)}, u32[]{:S(2)}, u32[]{:S(2)}) %all-to-all-start.8) | async-done | bytes 1572896 | tf_op jit(solution)/shard_map/all_to_all | solution.py:500
  718.7 2.7 copy.161
  721.3 2.7 copy.162
  (252 shorter events, 81.8 us)
Async XLA Ops:
  0.7 134.4 %copy-start = (bf16[768,2304]{1,0:T(8,128)(2,1)S(1)}, bf16[768,2304]{1,0:T(8,128)(2,1)}, u32[]{:S(2)}) copy-start(bf16[768,2304]{1,0:T(8,128)(2,1)} %param.28) | copy-start | bytes 10616836
  0.7 7.6 %copy-start.44 = (s32[8,128,2]{1,2,0:T(2,128)S(1)}, s32[8,128,2]{1,2,0:T(2,128)}, u32[]{:S(2)}) copy-start(s32[8,128,2]{1,2,0:T(2,128)} %param.34) | copy-start | bytes 24580
  0.7 44.8 %all-to-all-start = ((bf16[8,128,768]{2,1,0:T(8,128)(2,1)}), bf16[8,128,768]{2,1,0:T(8,128)(2,1)}, u32[]{:S(2)}, u32[]{:S(2)}) async-start(bf16[8,128,768]{2,1,0:T(8,128)(2,1)} %param.26), calls=%async_computation | async-start | bytes 3145728 | tf_op jit(solution)/shard_map/all_to_all | solution.py:500
  13.4 10.2 %copy-start.22 = (s32[8,128,2]{1,2,0:T(2,128)}, s32[8,128,2]{1,2,0:T(2,128)S(1)}, u32[]{:S(2)}) copy-start(s32[8,128,2]{1,2,0:T(2,128)S(1)} %compare_select_fusion.1) | copy-start | bytes 24580
  14.0 20.7 %collective-permute-start = (s32[2,128]{1,0:T(2,128)}, s32[2,128]{1,0:T(2,128)S(1)}, u32[]{:S(2)}, u32[]{:S(2)}) collective-permute-start(s32[2,128]{1,0:T(2,128)} %get-tuple-element.145), channel_id=1, source_target_pairs={{0,7},{1,0},{2,1},{3,2},{4,3},{5,4},{6,5},{7,6},{8,15},{9,8},{10,9... | collective-permute-start | bytes 3080 | tf_op jit(solution)/shard_map/ppermute | solution.py:513
  18.8 31.3 %collective-permute-start.1 = (s32[2,128]{1,0:T(2,128)}, s32[2,128]{1,0:T(2,128)}, u32[]{:S(2)}, u32[]{:S(2)}) collective-permute-start(s32[2,128]{1,0:T(2,128)} %get-tuple-element.144), channel_id=1, source_target_pairs={{0,6},{1,7},{2,0},{3,1},{4,2},{5,3},{6,4},{7,5},{8,14},{9,15},{10,... | collective-permute-start | bytes 3080 | tf_op jit(solution)/shard_map/ppermute | solution.py:513
  19.3 34.5 %collective-permute-start.2 = (s32[2,128]{1,0:T(2,128)}, s32[2,128]{1,0:T(2,128)}, u32[]{:S(2)}, u32[]{:S(2)}) collective-permute-start(s32[2,128]{1,0:T(2,128)} %get-tuple-element.143), channel_id=1, source_target_pairs={{0,5},{1,6},{2,7},{3,0},{4,1},{5,2},{6,3},{7,4},{8,13},{9,14},{10,... | collective-permute-start | bytes 3080 | tf_op jit(solution)/shard_map/ppermute | solution.py:513
  19.3 35.7 %collective-permute-start.3 = (s32[2,128]{1,0:T(2,128)}, s32[2,128]{1,0:T(2,128)}, u32[]{:S(2)}, u32[]{:S(2)}) collective-permute-start(s32[2,128]{1,0:T(2,128)} %get-tuple-element.142), channel_id=1, source_target_pairs={{0,4},{1,5},{2,6},{3,7},{4,0},{5,1},{6,2},{7,3},{8,12},{9,13},{10,... | collective-permute-start | bytes 3080 | tf_op jit(solution)/shard_map/ppermute | solution.py:513
  22.3 34.0 %collective-permute-start.4 = (s32[2,128]{1,0:T(2,128)}, s32[2,128]{1,0:T(2,128)}, u32[]{:S(2)}, u32[]{:S(2)}) collective-permute-start(s32[2,128]{1,0:T(2,128)} %get-tuple-element.141), channel_id=1, source_target_pairs={{0,3},{1,4},{2,5},{3,6},{4,7},{5,0},{6,1},{7,2},{8,11},{9,12},{10,... | collective-permute-start | bytes 3080 | tf_op jit(solution)/shard_map/ppermute | solution.py:513
  34.7 22.8 %collective-permute-start.5 = (s32[2,128]{1,0:T(2,128)}, s32[2,128]{1,0:T(2,128)S(1)}, u32[]{:S(2)}, u32[]{:S(2)}) collective-permute-start(s32[2,128]{1,0:T(2,128)} %get-tuple-element.140), channel_id=1, source_target_pairs={{0,2},{1,3},{2,4},{3,5},{4,6},{5,7},{6,0},{7,1},{8,10},{9,11},{10,... | collective-permute-start | bytes 3080 | tf_op jit(solution)/shard_map/ppermute | solution.py:513
  45.5 130.1 %all-to-all-start.1 = ((bf16[8,8,40,768]{3,2,1,0:T(8,128)(2,1)}), bf16[8,8,40,768]{3,2,1,0:T(8,128)(2,1)}, u32[]{:S(2)}, u32[]{:S(2)}) async-start(bf16[8,8,40,768]{3,2,1,0:T(8,128)(2,1)} %send_rows.3), calls=%async_computation.1 | async-start | bytes 7864320 | tf_op jit(solution)/shard_map/all_to_all | solution.py:564
  50.0 82.9 %copy-start.29 = (f32[768]{0:T(1024)S(1)}, f32[768]{0:T(1024)}, u32[]{:S(2)}) copy-start(f32[768]{0:T(1024)} %get-tuple-element.154) | copy-start | bytes 9220
  50.1 82.9 %copy-start.50 = (f32[768]{0:T(1024)S(1)}, f32[768]{0:T(1024)}, u32[]{:S(2)}) copy-start(f32[768]{0:T(1024)} %get-tuple-element.96) | copy-start | bytes 9220
  50.1 67.7 %collective-permute-start.6 = (s32[2,128]{1,0:T(2,128)}, s32[2,128]{1,0:T(2,128)S(1)}, u32[]{:S(2)}, u32[]{:S(2)}) collective-permute-start(s32[2,128]{1,0:T(2,128)} %get-tuple-element.139), channel_id=1, source_target_pairs={{0,1},{1,2},{2,3},{3,4},{4,5},{5,6},{6,7},{7,0},{8,9},{9,10},{10,1... | collective-permute-start | bytes 3080 | tf_op jit(solution)/shard_map/ppermute | solution.py:513
  128.7 72.6 %copy-start.23 = (s32[8,2,128]{2,1,0:T(2,128)}, s32[8,2,128]{2,1,0:T(2,128)S(1)}, u32[]{:S(2)}) copy-start(s32[8,2,128]{2,1,0:T(2,128)S(1)} %get-tuple-element.105) | copy-start | bytes 24580
  135.1 5.5 copy-start.11
  175.6 110.7 %all-to-all-start.2 = ((bf16[8,8,40,768]{3,2,1,0:T(8,128)(2,1)}), bf16[8,8,40,768]{3,2,1,0:T(8,128)(2,1)}, u32[]{:S(2)}, u32[]{:S(2)}) async-start(bf16[8,8,40,768]{3,2,1,0:T(8,128)(2,1)} %send_rows.2), calls=%async_computation.2 | async-start | bytes 7864320 | tf_op jit(solution)/shard_map/all_to_all | solution.py:564
  198.6 3.9 copy-start.35
  198.6 4.4 copy-start.39
  286.4 71.2 %all-to-all-start.3 = ((bf16[8,128,768]{2,1,0:T(8,128)(2,1)}), bf16[8,128,768]{2,1,0:T(8,128)(2,1)}, u32[]{:S(2)}, u32[]{:S(2)}) async-start(bf16[8,128,768]{2,1,0:T(8,128)(2,1)} %param.27), calls=%async_computation.3 | async-start | bytes 3145728 | tf_op jit(solution)/shard_map/all_to_all | solution.py:500
  357.5 91.3 %all-to-all-start.4 = ((bf16[8,8,40,768]{3,2,1,0:T(8,128)(2,1)}), bf16[8,8,40,768]{3,2,1,0:T(8,128)(2,1)}, u32[]{:S(2)}, u32[]{:S(2)}) async-start(bf16[8,8,40,768]{3,2,1,0:T(8,128)(2,1)} %bitcast.240), calls=%async_computation.4 | async-start | bytes 7864320 | tf_op jit(solution)/shard_map/all_to_all | solution.py:564
  386.1 45.6 %collective-permute-start.8 = (bf16[768,768]{1,0:T(8,128)(2,1)}, bf16[768,768]{1,0:T(8,128)(2,1)}, u32[]{:S(2)}, u32[]{:S(2)}) collective-permute-start(bf16[768,768]{1,0:T(8,128)(2,1)} %get-tuple-element.117), channel_id=1, source_target_pairs={{0,8},{8,0},{16,24},{24,16},{1,9},{9,1},{17,25},{25,17},{2,10},{10... | collective-permute-start | bytes 3538952 | tf_op jit(solution)/shard_map/ppermute | solution.py:530
  386.1 18.6 %copy-start.10 = (bf16[1,8,8,40,768]{4,3,2,1,0:T(8,128)(2,1)S(1)}, bf16[1,8,8,40,768]{4,3,2,1,0:T(8,128)(2,1)}, u32[]{:S(2)}) copy-start(bf16[1,8,8,40,768]{4,3,2,1,0:T(8,128)(2,1)} %copy-done.9) | copy-start | bytes 11796484
  386.1 18.6 %copy-start.58 = (f32[2560]{0:T(1024)S(1)}, f32[2560]{0:T(1024)}, u32[]{:S(2)}) copy-start(f32[2560]{0:T(1024)} %mul.334) | copy-start | bytes 30724
  386.1 45.6 %collective-permute-start.7 = (bf16[768,768]{1,0:T(8,128)(2,1)}, bf16[768,768]{1,0:T(8,128)(2,1)}, u32[]{:S(2)}, u32[]{:S(2)}) collective-permute-start(bf16[768,768]{1,0:T(8,128)(2,1)} %get-tuple-element.118), channel_id=1, source_target_pairs={{0,8},{8,0},{16,24},{24,16},{1,9},{9,1},{17,25},{25,17},{2,10},{10... | collective-permute-start | bytes 3538952 | tf_op jit(solution)/shard_map/ppermute | solution.py:530
  429.2 6.9 collective-permute-start.10
  429.3 6.9 collective-permute-start.9
  431.7 4.5 copy-start.8
  436.2 12.7 %copy-start.37 = (s32[8,1,128]{2,1,0:T(1,128)S(1)}, s32[8,1,128]{2,1,0:T(1,128)}, u32[]{:S(2)}) copy-start(s32[8,1,128]{2,1,0:T(1,128)} %copy-done.35) | copy-start | bytes 12292
  438.4 13.9 %copy-start.26 = (f32[1024]{0:T(1024)S(1)}, f32[1024]{0:T(1024)}, u32[]{:S(2)}) copy-start(f32[1024]{0:T(1024)} %copy-done.25) | copy-start | bytes 12292
  448.9 3.4 copy-start.20
  459.0 129.9 %all-to-all-start.5 = ((bf16[8,8,40,768]{3,2,1,0:T(8,128)(2,1)}), bf16[8,8,40,768]{3,2,1,0:T(8,128)(2,1)}, u32[]{:S(2)}, u32[]{:S(2)}) async-start(bf16[8,8,40,768]{3,2,1,0:T(8,128)(2,1)} %bitcast.237), calls=%async_computation.5 | async-start | bytes 7864320 | tf_op jit(solution)/shard_map/all_to_all | solution.py:564
  464.5 3.9 copy-start.61
  512.5 8.2 %copy-start.16 = (bf16[1024,2304]{1,0:T(8,128)(2,1)}, bf16[1024,2304]{1,0:T(8,128)(2,1)S(1)}, u32[]{:S(2)}) copy-start(bf16[1024,2304]{1,0:T(8,128)(2,1)S(1)} %constant_dynamic-update-slice_fusion.16) | copy-start | bytes 14155780
  512.5 8.2 %copy-start.59 = (bf16[768]{0:T(1024)(128)(2,1)S(1)}, bf16[768]{0:T(1024)(128)(2,1)}, u32[]{:S(2)}) copy-start(bf16[768]{0:T(1024)(128)(2,1)} %get-tuple-element.83) | copy-start | bytes 4612
  512.5 8.3 %copy-start.57 = (bf16[1,768]{1,0:T(2,128)(2,1)S(1)}, bf16[1,768]{1,0:T(2,128)(2,1)}, u32[]{:S(2)}) copy-start(bf16[1,768]{1,0:T(2,128)(2,1)} %stack.65) | copy-start | bytes 4612
  512.5 8.3 %copy-start.27 = (bf16[768,8]{0,1:T(8,128)(2,1)S(1)}, bf16[768,8]{0,1:T(8,128)(2,1)}, u32[]{:S(2)}) copy-start(bf16[768,8]{0,1:T(8,128)(2,1)} %convolution_convert_fusion.8) | copy-start | bytes 36868
  523.0 4.0 copy-start.12
  523.0 4.2 copy-start.17
  527.2 4.4 copy-start.15
  535.0 60.0 %collective-permute-start.12 = (bf16[192,3200]{1,0:T(8,128)(2,1)}, bf16[192,3200]{1,0:T(8,128)(2,1)}, u32[]{:S(2)}, u32[]{:S(2)}) collective-permute-start(bf16[192,3200]{1,0:T(8,128)(2,1)} %get-tuple-element.109), channel_id=1, source_target_pairs={{0,8},{8,0},{16,24},{24,16},{1,9},{9,1},{17,25},{25,17},{2,10},{10... | collective-permute-start | bytes 3686408 | tf_op jit(solution)/shard_map/ppermute | solution.py:530
  535.0 60.0 %collective-permute-start.11 = (bf16[192,3200]{1,0:T(8,128)(2,1)}, bf16[192,3200]{1,0:T(8,128)(2,1)}, u32[]{:S(2)}, u32[]{:S(2)}) collective-permute-start(bf16[192,3200]{1,0:T(8,128)(2,1)} %get-tuple-element.110), channel_id=1, source_target_pairs={{0,8},{8,0},{16,24},{24,16},{1,9},{9,1},{17,25},{25,17},{2,10},{10... | collective-permute-start | bytes 3686408 | tf_op jit(solution)/shard_map/ppermute | solution.py:530
  535.5 29.2 %collective-permute-start.14 = (bf16[768,768]{1,0:T(8,128)(2,1)}, bf16[768,768]{1,0:T(8,128)(2,1)}, u32[]{:S(2)}, u32[]{:S(2)}) collective-permute-start(bf16[768,768]{1,0:T(8,128)(2,1)} %get-tuple-element.115), channel_id=1, source_target_pairs={{0,16},{8,24},{16,0},{24,8},{1,17},{9,25},{17,1},{25,9},{2,18},{10... | collective-permute-start | bytes 3538952 | tf_op jit(solution)/shard_map/ppermute | solution.py:527
  536.9 52.0 %collective-permute-start.15 = (bf16[768,768]{1,0:T(8,128)(2,1)}, bf16[768,768]{1,0:T(8,128)(2,1)}, u32[]{:S(2)}, u32[]{:S(2)}) collective-permute-start(bf16[768,768]{1,0:T(8,128)(2,1)} %get-tuple-element.111), channel_id=1, source_target_pairs={{0,16},{8,24},{16,0},{24,8},{1,17},{9,25},{17,1},{25,9},{2,18},{10... | collective-permute-start | bytes 3538952 | tf_op jit(solution)/shard_map/ppermute | solution.py:527
  589.0 44.7 %all-to-all-start.6 = ((bf16[8,128,768]{2,1,0:T(8,128)(2,1)}), bf16[8,128,768]{2,1,0:T(8,128)(2,1)}, u32[]{:S(2)}, u32[]{:S(2)}) async-start(bf16[8,128,768]{2,1,0:T(8,128)(2,1)} %bitcast.236), calls=%async_computation.6 | async-start | bytes 3145728 | tf_op jit(solution)/shard_map/all_to_all | solution.py:500
  594.9 4.6 copy-start.62
  594.9 5.2 copy-start.38
  594.9 5.2 copy-start.41
  595.0 5.2 copy-start.52
  595.0 5.2 copy-start.54
  595.0 5.2 copy-start.60
  598.0 27.9 %collective-permute-start.13 = (bf16[192,3200]{1,0:T(8,128)(2,1)S(1)}, bf16[192,3200]{1,0:T(8,128)(2,1)S(1)}, u32[]{:S(2)}, u32[]{:S(2)}) collective-permute-start(bf16[192,3200]{1,0:T(8,128)(2,1)S(1)} %get-tuple-element.107), channel_id=1, source_target_pairs={{0,16},{8,24},{16,0},{24,8},{1,17},{9,25},{17,1},{25,9},{2,18},{10... | collective-permute-start | bytes 3686408 | tf_op jit(solution)/shard_map/ppermute | solution.py:527
  633.7 34.7 %all-to-all-start.7 = ((bf16[8,208,384]{2,1,0:T(8,128)(2,1)}), bf16[8,208,384]{2,1,0:T(8,128)(2,1)}, u32[]{:S(2)}, u32[]{:S(2)}) async-start(bf16[8,208,384]{2,1,0:T(8,128)(2,1)} %deal.1), calls=%async_computation.7 | async-start | bytes 2555904 | tf_op jit(solution)/shard_map/all_to_all | solution.py:564
  670.6 5.6 collective-permute-start.17
  672.0 8.8 %collective-permute-start.16 = (bf16[208,384]{1,0:T(8,128)(2,1)}, bf16[208,384]{1,0:T(8,128)(2,1)}, u32[]{:S(2)}, u32[]{:S(2)}) collective-permute-start(bf16[208,384]{1,0:T(8,128)(2,1)} %reduce_sum.242), channel_id=1, source_target_pairs={{0,8},{8,0},{16,24},{24,16},{1,9},{9,1},{17,25},{25,17},{2,10},{10... | collective-permute-start | bytes 479240 | tf_op jit(solution)/shard_map/ppermute | solution.py:530
  676.2 4.7 collective-permute-start.18
  676.2 42.5 %all-to-all-start.8 = ((bf16[8,128,768]{2,1,0:T(8,128)(2,1)}), bf16[8,128,768]{2,1,0:T(8,128)(2,1)}, u32[]{:S(2)}, u32[]{:S(2)}) async-start(bf16[8,128,768]{2,1,0:T(8,128)(2,1)} %bitcast.235), calls=%async_computation.8 | async-start | bytes 3145728 | tf_op jit(solution)/shard_map/all_to_all | solution.py:500
  680.8 5.3 copy-start.47
  680.8 5.3 copy-start.48
  680.8 5.2 copy-start.55
  680.8 5.2 copy-start.56
  680.8 5.9 copy-start.21
  680.8 5.9 copy-start.45
  680.8 5.9 copy-start.46
  (27 other events, 56.4 us)
